TPU v7x, 256 devices: a whole 4x4x8 slice. The times are simulated.
256 devices in a mesh: ctx: 64 (over y, z, core), head: 4 (over x).
Axes of the slice: x: 4, y: 4, z: 8, core: 2. Of those that a mesh axis runs over, the one named last changes fastest.
Arguments:
- block_order: int32 [128], replicated, may hold values from 0 to 127, as said below
- main_query: bfloat16 [8192, 36864], P('ctx', 'head'), may hold values from -256 to 256
- latent_key: bfloat16 [576, 8192], P(None, 'ctx'), may hold values from -24 to 24
- index_query: bfloat16 [8192, 32, 128], P('ctx', 'head'), may hold values from -64 to 64
- index_weight: bfloat16 [8192, 32], P('ctx', 'head'), may hold values from -0.6 to 0.6
- index_key: bfloat16 [128, 8192], P(None, 'ctx'), may hold values from -24 to 24
Outputs:
- row_loss: float32 [8192], P('ctx')
- grad_query: bfloat16 [8192, 32, 128], P('ctx', 'head')
- grad_weight: bfloat16 [8192, 32], P('ctx', 'head')
- grad_key: float32 [8192, 128], P(('ctx', 'head'))
Inputs may be any that keep to these rules, and one draw needn't show every extreme that they name: `block_order`: slots 2d and 2d+1 hold blocks s * 64 + c and s * 64 + 128 // 2 - 1 - c of one sequence s, for some c below 32, and every block appears once.
All inputs are finite; a program needn't handle non-finite values.
Results may differ from a plain program's by a relative error of at most 0.01.
Values may be sent and summed in bfloat16 or wider, within the bound.
No kernel may reach another device: no remote copies, remote signals or barrier semaphores. Data moves between devices by JAX's collectives and lax.ppermute only.
A program may use at most 128 MiB of HBM per device.

v0:
```python
import math

import jax
import jax.numpy as jnp
from jax import lax
from jax.experimental import pallas as pl
from jax.experimental.pallas import tpu as pltpu
from jax.sharding import Mesh
from jax.sharding import PartitionSpec as P


HM = 64
HI = 32
DI = 128
KW = 576
HEAD_QK = 192
BLOCK = 64
LENGTH = 4096
HALF = LENGTH // 2
CTX = ("ctx_0", "ctx_1", "ctx_2")
CTX_HEAD = ("ctx_0", "ctx_1", "ctx_2", "head")
HEADS = 4
GROUP = 16
MAIN_LANES = HM // HEADS * KW
INDEX_LANES = HI // HEADS * DI
ALL_LANES = MAIN_LANES + INDEX_LANES + 128
TILE = 256
TILES = LENGTH // TILE
WIDE = 512
ROWS = HM * GROUP
IROWS = HI * GROUP
KEY_ROWS = 1024
GRAD_ROWS = 9 * 2 * GROUP
HALF_ROWS = (KW + DI) // 2
STRIP = 208
STRIP_CUT = 112
REST = HALF_ROWS - STRIP
REST_CUT = 80
PIECES = 14
masked_value = -1e30
SCORE_EXP2 = math.log2(math.e) / math.sqrt(HEAD_QK)
f32 = jnp.float32
bf16 = jnp.bfloat16


def sources(y, z):
    if y == 2:
        first = [(3, 0, STRIP_CUT), (4, STRIP_CUT, STRIP - STRIP_CUT)]
    else:
        first = [({0: 0, 1: 1, 3: 2}[y], 0, STRIP)]
    if z == 4:
        rest = [(12, STRIP, REST_CUT), (13, STRIP + REST_CUT, REST - REST_CUT)]
    else:
        rest = [({0: 5, 1: 6, 2: 7, 3: 8, 5: 9, 6: 10, 7: 11}[z], STRIP, REST)]
    return first, rest


def nt_dot(a, b):
    return lax.dot_general(a, b, (((1,), (1,)), ((), ())), preferred_element_type=f32)


def own_block(order_ref):
    y, z, core = (lax.axis_index(axis) for axis in CTX)
    own = order_ref[((y * 8 + z) * 2 + core) * 2]
    first = jnp.where(own >= 64, 64, 0)
    return first, own - first


def rows_kernel(order_ref, *refs):
    pieces = refs[: 2 * PIECES]
    q_ref, out_ref = refs[2 * PIECES : 2 * PIECES + 2]
    (
        raw, keys, q_all, qi_all, scores, best, total, w_all, target, logits, slope, gsum,
        key_grad, sems,
    ) = refs[2 * PIECES + 2 :]
    y_own, z_own, core_own = (lax.axis_index(axis) for axis in CTX)
    h_own = lax.axis_index("head")
    first, c_own = own_block(order_ref)
    own_half = pl.multiple_of(core_own * HALF_ROWS, 16)
    other_half = pl.multiple_of((1 - core_own) * HALF_ROWS, 16)

    for y in range(4):
        for z in range(8):
            for core in range(2):
                y_from, z_from = (y_own + y) % 4, (z_own + z) % 8
                place = (y_from * 8 + z_from) * 2 + (core_own + core) % 2
                slot = order_ref[2 * place] - first

                @pl.when((slot >= 0) & (slot < 64))
                def _():
                    for parts, block in zip(sources(y, z), (z_from, y)):
                        for piece, at, size in parts:
                            for kind, half in ((0, own_half), (1, other_half)):
                                pltpu.make_async_copy(
                                    pieces[kind * PIECES + piece].at[block, core ^ kind],
                                    raw.at[slot, pl.ds(half + at, size), :],
                                    sems.at[slot],
                                ).start()

    def arrived(n):
        pltpu.make_async_copy(raw.at[n], raw.at[n], sems.at[n]).wait()

    keys[0:64, :] = jnp.zeros((64, LENGTH), bf16)
    keys[640:704, :] = jnp.zeros((64, LENGTH), bf16)

    for e in range(2):
        for src in range(HEADS):
            for i in range(8):
                at = (src * 8 + i) * GROUP
                for parity in range(2):
                    lane = i * 2 * KW + parity * (KW - 64)
                    q_all[e, parity, at : at + GROUP, :] = q_ref[src, e, :, lane : lane + 640]
                lane = MAIN_LANES + i * DI
                qi_all[e, at : at + GROUP, :] = q_ref[src, e, :, lane : lane + DI]
                lane = MAIN_LANES + INDEX_LANES
                column = q_ref[src, e, :, lane : lane + 128].astype(f32)[:, i : i + 1]
                w_all[e, at : at + GROUP, :] = jnp.broadcast_to(column, (GROUP, DI))

    take = lax.broadcasted_iota(jnp.int32, (256, 256), 0)
    give = lax.broadcasted_iota(jnp.int32, (256, 256), 1)
    source = jnp.where(give // 64 == 1, give + 64, jnp.where(give // 64 == 2, give - 64, give))
    shuffle = jnp.where(take == source, 1.0, 0.0).astype(bf16)

    def sort_pair(i, carry):
        arrived(2 * i)
        arrived(2 * i + 1)
        both = jnp.concatenate([raw[2 * i], raw[2 * i + 1]], axis=1)
        mixed = jnp.dot(both, shuffle, preferred_element_type=f32).astype(bf16)
        early = pl.multiple_of(i * 128, 128)
        late = pl.multiple_of(HALF + i * 128, 128)
        keys[64:640, pl.ds(early, 128)] = mixed[0:KW, 0:128]
        keys[704:832, pl.ds(early, 128)] = mixed[KW:, 0:128]
        keys[64:640, pl.ds(late, 128)] = mixed[0:KW, 128:256]
        keys[704:832, pl.ds(late, 128)] = mixed[KW:, 128:256]
        return carry

    lax.fori_loop(0, 16, sort_pair, 0)

    key_grad[...] = jnp.zeros((DI, LENGTH), f32)

    for e in range(2):
        row_pos = lax.broadcasted_iota(jnp.int32, (GROUP, 1), 0) + h_own * GROUP
        row_pos = row_pos + (c_own if e == 0 else 63 - c_own) * BLOCK

        def key_pos(at, width):
            lane = lax.broadcasted_iota(jnp.int32, (1, width), 1) + at
            late_lane = lane - HALF
            late_pos = (63 - late_lane // BLOCK) * BLOCK + late_lane % BLOCK
            return jnp.where(lane < HALF, lane, late_pos)

        early_tiles = c_own // 4 + 1 if e == 0 else TILES // 2
        late_tiles = 0 if e == 0 else TILES // 2 - c_own // 4

        def tile_at(j):
            if e == 0:
                return pl.multiple_of(j * TILE, TILE)
            return pl.multiple_of(jnp.where(j < TILES // 2, j, j + c_own // 4) * TILE, TILE)

        steps = early_tiles + late_tiles

        best[...] = jnp.full((ROWS, 128), masked_value, f32)
        total[...] = jnp.zeros((ROWS, 128), f32)
        target[...] = jnp.zeros((GROUP, LENGTH), f32)
        logits[...] = jnp.full((GROUP, LENGTH), masked_value, f32)

        wide_steps = c_own // 8 + 1 if e == 0 else LENGTH // WIDE - c_own // 8

        def score_step(j, carry):
            at = j if e == 0 else jnp.where(j < HALF // WIDE, j, j + c_own // 8)
            at = pl.multiple_of(at * WIDE, WIDE)
            visible = key_pos(at, WIDE) <= row_pos
            for parity in range(2):
                k = keys[64 * (1 - parity) : 64 * (1 - parity) + 640, pl.ds(at, WIDE)]
                s = jnp.dot(q_all[e, parity], k, preferred_element_type=f32)
                s = jnp.where(visible[None], s.reshape(HM // 2, GROUP, WIDE), masked_value)
                s = s.reshape(ROWS // 2, WIDE)
                r = slice(parity * (ROWS // 2), (parity + 1) * (ROWS // 2))
                scores[r, pl.ds(at, WIDE)] = s
                top = jnp.maximum(s[:, 0:128], s[:, 128:256])
                best[r] = jnp.maximum(best[r], jnp.maximum(top, jnp.maximum(s[:, 256:384], s[:, 384:512])))
            return carry

        lax.fori_loop(0, wide_steps, score_step, 0)

        def top_step(g, carry):
            r = pl.ds(pl.multiple_of(g * 128, 128), 128)
            best[r] = jnp.broadcast_to(jnp.max(best[r], axis=1, keepdims=True), (128, 128))
            return carry

        lax.fori_loop(0, ROWS // 128, top_step, 0)

        def exp_step(j, carry):
            at = tile_at(j)
            for g in range(ROWS // 128):
                r = slice(g * 128, (g + 1) * 128)
                top = best[r]
                part = total[r]
                for half in range(TILE // 128):
                    lanes = pl.ds(pl.multiple_of(at + half * 128, 128), 128)
                    raised = jnp.exp2((scores[r, lanes] - top) * SCORE_EXP2)
                    scores[r, lanes] = raised
                    part = part + raised
                total[r] = part
            return carry

        lax.fori_loop(0, steps, exp_step, 0)

        def total_step(g, carry):
            r = pl.ds(pl.multiple_of(g * 128, 128), 128)
            whole = jnp.sum(total[r], axis=1, keepdims=True)
            total[r] = jnp.broadcast_to((1.0 / HM) / whole, (128, 128))
            return carry

        lax.fori_loop(0, ROWS // 128, total_step, 0)

        def index_logits(at):
            act = jnp.dot(
                qi_all[e], keys[704:832, pl.ds(at, TILE)], preferred_element_type=f32
            )
            out = jnp.zeros((GROUP, TILE), f32)
            for h in range(HI):
                r = slice(h * GROUP, (h + 1) * GROUP)
                w = w_all[e, r]
                out = out + jnp.maximum(act[r], 0.0) * jnp.concatenate([w, w], axis=1)
            return out

        def target_step(j, carry):
            at = tile_at(j)
            lanes = pl.ds(at, TILE)
            acc = jnp.zeros((GROUP, TILE), f32)
            for h in range(HM):
                r = slice(h * GROUP, (h + 1) * GROUP)
                share = total[r]
                acc = acc + scores[r, lanes] * jnp.concatenate([share, share], axis=1)
            target[:, lanes] = acc
            visible = key_pos(at, TILE) <= row_pos
            logits[:, lanes] = jnp.where(visible, index_logits(at), masked_value)
            return carry

        lax.fori_loop(0, steps, target_step, 0)

        masked = logits[...]
        visible = masked > 0.5 * masked_value
        top_logit = jnp.max(masked, axis=1, keepdims=True)
        lse = top_logit + jnp.log(jnp.sum(jnp.exp(masked - top_logit), axis=1, keepdims=True))
        loss = jnp.sum(jnp.where(visible, target[...] * (lse - masked), 0.0), axis=1, keepdims=True)
        rounded = jnp.where(visible, jnp.exp(masked - lse) - target[...], 0.0).astype(bf16)
        slope[...] = rounded.astype(f32)

        gsum[...] = jnp.zeros((IROWS, DI), f32)
        q_float = qi_all[e].astype(f32)
        weighted = jnp.transpose(q_float * w_all[e]).astype(bf16)

        def back_step(j, carry):
            at = j if e == 0 else jnp.where(j < HALF // WIDE, j, j + c_own // 8)
            lanes = pl.ds(pl.multiple_of(at * WIDE, WIDE), WIDE)
            k = keys[704:832, lanes]
            act = jnp.dot(qi_all[e], k, preferred_element_type=f32)
            through = jnp.where(
                act.reshape(HI, GROUP, WIDE) > 0.0, slope[:, lanes][None], 0.0
            ).reshape(IROWS, WIDE).astype(bf16)
            gsum[...] += nt_dot(through, k)
            key_grad[:, lanes] += jnp.dot(weighted, through, preferred_element_type=f32)
            return carry

        lax.fori_loop(0, wide_steps, back_step, 0)

        grads = (gsum[...] * w_all[e]).astype(bf16)
        column = jnp.sum(gsum[...] * q_float, axis=1, keepdims=True)
        lane = lax.broadcasted_iota(jnp.int32, (GROUP, 128), 1)
        high = loss.astype(bf16).astype(f32)
        middle = (loss - high).astype(bf16).astype(f32)
        low = loss - high - middle
        extra = jnp.where(lane == 8, high, jnp.where(lane == 9, middle, jnp.where(lane == 10, low, 0.0)))
        for dst in range(HEADS):
            small = extra
            for i in range(8):
                at = (dst * 8 + i) * GROUP
                to = KEY_ROWS + (e * 9 + i) * GROUP
                out_ref[dst, to : to + GROUP, :] = grads[at : at + GROUP]
                small = jnp.where(lane == i, column[at : at + GROUP], small)
            to = KEY_ROWS + (e * 9 + 8) * GROUP
            out_ref[dst, to : to + GROUP, :] = small.astype(bf16)

    def emit(i, carry):
        for late in range(2):
            lanes = pl.ds(pl.multiple_of(late * HALF + i * 128, 128), 128)
            turned = jnp.transpose(key_grad[:, lanes]).astype(bf16)
            for k in range(4):
                to = pl.multiple_of(i * 64 + (k // 2) * 32, 32)
                out_ref[2 * late + k % 2, pl.ds(to, 32), :] = turned[k * 32 : (k + 1) * 32]
        return carry

    lax.fori_loop(0, 16, emit, 0)


def rows_call(order, pieces, queries):
    return pl.pallas_call(
        rows_kernel,
        out_shape=jax.ShapeDtypeStruct((HEADS, KEY_ROWS + GRAD_ROWS, DI), bf16),
        in_specs=[
            pl.BlockSpec(memory_space=pltpu.SMEM),
            *[pl.BlockSpec(memory_space=pl.ANY)] * (2 * PIECES),
            pl.BlockSpec(memory_space=pltpu.VMEM),
        ],
        out_specs=pl.BlockSpec(memory_space=pltpu.VMEM),
        scratch_shapes=[
            pltpu.VMEM((32, KW + DI, 128), bf16),
            pltpu.VMEM((832, LENGTH), bf16),
            pltpu.VMEM((2, 2, ROWS // 2, 640), bf16),
            pltpu.VMEM((2, IROWS, DI), bf16),
            pltpu.VMEM((ROWS, LENGTH), f32),
            pltpu.VMEM((ROWS, 128), f32),
            pltpu.VMEM((ROWS, 128), f32),
            pltpu.VMEM((2, IROWS, DI), f32),
            pltpu.VMEM((GROUP, LENGTH), f32),
            pltpu.VMEM((GROUP, LENGTH), f32),
            pltpu.VMEM((GROUP, LENGTH), f32),
            pltpu.VMEM((IROWS, DI), f32),
            pltpu.VMEM((DI, LENGTH), f32),
            pltpu.SemaphoreType.DMA((32,)),
        ],
        compiler_params=pltpu.CompilerParams(vmem_limit_bytes=58 * 1024 * 1024),
        name="rows_work",
    )(order, *pieces, queries)


def spread_kernel(order_ref, got_ref, out_ref, sums):
    first, _ = own_block(order_ref)
    total = got_ref[0, 0:KEY_ROWS].astype(f32)
    for src in range(1, HEADS):
        total = total + got_ref[src, 0:KEY_ROWS].astype(f32)
    sums[0:KEY_ROWS] = total.astype(bf16)
    sums[KEY_ROWS:] = jnp.zeros((32, DI), bf16)

    def put(d, carry):
        slot = order_ref[2 * d] - first
        slot = jnp.where((slot >= 0) & (slot < 64), slot, 32)
        out_ref[d] = sums[pl.ds(pl.multiple_of(slot * 32, 32), 32)]
        return carry

    lax.fori_loop(0, 64, put, 0, unroll=8)


def spread_call(order, got):
    return pl.pallas_call(
        spread_kernel,
        out_shape=jax.ShapeDtypeStruct((64, 32, DI), bf16),
        in_specs=[
            pl.BlockSpec(memory_space=pltpu.SMEM),
            pl.BlockSpec(memory_space=pltpu.VMEM),
        ],
        out_specs=pl.BlockSpec(memory_space=pltpu.VMEM),
        scratch_shapes=[pltpu.VMEM((KEY_ROWS + 32, DI), bf16)],
        name="spread_keys",
    )(order, got)


def work(block_order, main_query, latent_key, index_query, index_weight, index_key):
    shard = jnp.concatenate([latent_key, index_key], axis=0)
    pieces = gather_keys(shard)

    weights = jnp.pad(index_weight, ((0, 0), (0, 128 - index_weight.shape[1])))
    rows = jnp.concatenate([main_query, index_query.reshape(128, INDEX_LANES), weights], axis=1)
    rows = rows.reshape(2, HEADS, GROUP, ALL_LANES).swapaxes(0, 1)
    queries = lax.all_to_all(rows, "head", split_axis=0, concat_axis=0, tiled=True)

    sent = rows_call(block_order, pieces, queries)
    got = lax.all_to_all(sent, "head", split_axis=0, concat_axis=0, tiled=True)
    parts = lax.all_to_all(spread_call(block_order, got), CTX, split_axis=0, concat_axis=0, tiled=True)
    grad_key = jnp.sum(parts.astype(f32), axis=0)

    grads = got[:, KEY_ROWS:].reshape(HEADS, 2, 9, GROUP, DI).transpose(1, 0, 3, 2, 4)
    grads = grads.reshape(128, 9, DI)
    small = grads[:, 8]
    row_loss = jnp.sum(small[:, 8:11].astype(f32), axis=1)
    return (row_loss, grads[:, 0:8], small[:, 0:8], grad_key)


def onward(piece, axis):
    n = lax.axis_size(axis)
    return lax.ppermute(piece, axis, [(i, (i + 1) % n) for i in range(n)])


def backward(piece, axis):
    n = lax.axis_size(axis)
    return lax.ppermute(piece, axis, [(i, (i - 1) % n) for i in range(n)])


def swapped(piece):
    return lax.ppermute(piece, "ctx_2", [(0, 1), (1, 0)])


def sent_to_all(piece, axis):
    copies = jnp.broadcast_to(piece, (lax.axis_size(axis), *piece.shape))
    return lax.all_to_all(copies, axis, split_axis=0, concat_axis=0, tiled=True)


def gather_keys(shard):
    core = lax.axis_index("ctx_2")
    top, bottom = shard[:HALF_ROWS], shard[HALF_ROWS:]
    mine = jnp.where(core == 0, top, bottom)
    given = jnp.where(core == 0, bottom, top)
    block = jnp.stack([mine, swapped(given)])
    first, second = block[:, :STRIP], block[:, STRIP:]

    z, y = "ctx_1", "ctx_0"
    planes = sent_to_all(first, z)
    h1, g1 = backward(second, y), onward(second, y)
    g2 = lax.ppermute(second, y, [(i, (i + 2) % 4) for i in range(4)])
    rows = jnp.stack([second, h1, g2, g1])
    b1, f1 = backward(rows, z), onward(rows, z)
    down1, up1 = backward(planes, y), onward(planes, y)
    b2, f2 = backward(b1, z), onward(f1, z)
    up2, down2 = onward(up1[:, :, :STRIP_CUT], y), backward(down1[:, :, STRIP_CUT:], y)
    b3, f3 = backward(b2, z), onward(f2, z)
    f4, b4 = onward(f3[:, :, :REST_CUT], z), backward(b3[:, :, REST_CUT:], z)
    own = [planes, down1, up1, up2, down2, rows, b1, b2, b3, f3, f2, f1, f4, b4]
    return own + [swapped(piece) for piece in own]


def solution(mesh):
    split = Mesh(
        mesh.devices.reshape(4, 8, 2, mesh.shape["head"]), ("ctx_0", "ctx_1", "ctx_2", "head")
    )
    in_specs = (
        P(),
        P(CTX, "head"),
        P(None, CTX),
        P(CTX, "head", None),
        P(CTX, "head"),
        P(None, CTX),
    )
    out_specs = (P(CTX), P(CTX, "head", None), P(CTX, "head"), P(CTX_HEAD, None))
    return jax.shard_map(work, mesh=split, in_specs=in_specs, out_specs=out_specs, check_vma=False)
```

profile of v0, /device:TPU:8, one launch (start us, length us, event | category | flops | bytes accessed | tf_op | source)
XLA Modules:
  0.0 188.2 jit_solution(4687963451856035963)
XLA Ops:
  0.7 1.1 broadcast_select_fusion
  1.9 1.3 collective-permute-done
  3.2 2.2 %collective-permute-start.5 = (bf16[2,144,128]{2,1,0:T(8,128)(2,1)S(1)}, bf16[2,144,128]{2,1,0:T(8,128)(2,1)S(1)}, u32[]{:S(2)}, u32[]{:S(2)}) collective-permute-start(bf16[2,144,128]{2,1,0:T(8,128)(2,1)S(1)} %pad_maximum_fusion.3), channel_id=1, source_target_pairs={{0,192},{64,0},{128,64},{192,128},{1,193},{65,1},{129,65},{193,129... | collective-permute-start | bytes 221192 | tf_op jit(solution)/shard_map/ppermute | solution.py:387
  6.2 1.9 %collective-permute-start.7 = (bf16[2,144,128]{2,1,0:T(8,128)(2,1)S(1)}, bf16[2,144,128]{2,1,0:T(8,128)(2,1)S(1)}, u32[]{:S(2)}, u32[]{:S(2)}) collective-permute-start(bf16[2,144,128]{2,1,0:T(8,128)(2,1)S(1)} %pad_maximum_fusion.3), channel_id=1, source_target_pairs={{0,64},{64,128},{128,192},{192,0},{1,65},{65,129},{129,193},{193,1... | collective-permute-start | bytes 221192 | tf_op jit(solution)/shard_map/ppermute | solution.py:382
  8.1 3.1 %collective-permute-done.6 = bf16[2,144,128]{2,1,0:T(8,128)(2,1)S(1)} collective-permute-done((bf16[2,144,128]{2,1,0:T(8,128)(2,1)S(1)}, bf16[2,144,128]{2,1,0:T(8,128)(2,1)S(1)}, u32[]{:S(2)}, u32[]{:S(2)}) %collective-permute-start.6) | collective-permute-done | bytes 73760 | tf_op jit(solution)/shard_map/ppermute | solution.py:410
  11.9 1.6 collective-permute-start.11
  13.5 3.9 %collective-permute-start.8 = (bf16[4,2,144,128]{3,2,1,0:T(8,128)(2,1)}, bf16[4,2,144,128]{3,2,1,0:T(8,128)(2,1)}, u32[]{:S(2)}, u32[]{:S(2)}) collective-permute-start(bf16[4,2,144,128]{3,2,1,0:T(8,128)(2,1)} %pad_maximum_fusion.1.refs_5_), channel_id=1, source_target_pairs={{0,56},{8,0},{16,8},{24,16},{32,24},{40,32},{48,40},{56,48},{1,57}... | collective-permute-start | bytes 884744 | tf_op jit(solution)/shard_map/ppermute | solution.py:387
  18.5 5.8 %all-to-all-start = ((bf16[8,2,208,128]{3,2,1,0:T(8,128)(2,1)}), bf16[8,2,208,128]{3,2,1,0:T(8,128)(2,1)S(1)}, u32[]{:S(2)}, u32[]{:S(2)}) async-start(bf16[8,2,208,128]{3,2,1,0:T(8,128)(2,1)} %broadcast_in_dim.3), calls=%async_computation | async-start | bytes 1703936 | tf_op jit(solution)/shard_map/all_to_all | solution.py:396
  26.2 3.2 %collective-permute-start.9 = (bf16[4,2,144,128]{3,2,1,0:T(8,128)(2,1)}, bf16[4,2,144,128]{3,2,1,0:T(8,128)(2,1)}, u32[]{:S(2)}, u32[]{:S(2)}) collective-permute-start(bf16[4,2,144,128]{3,2,1,0:T(8,128)(2,1)} %collective-permute-done.8.refs_6_), channel_id=1, source_target_pairs={{0,56},{8,0},{16,8},{24,16},{32,24},{40,32},{48,40},{56,48},{1,57}... | collective-permute-start | bytes 884744 | tf_op jit(solution)/shard_map/ppermute | solution.py:387
  29.4 1.7 copy_bitcast_fusion
  31.1 16.4 %all-to-all-done.refs_0_ = bf16[8,2,208,128]{3,2,1,0:T(8,128)(2,1)S(1)} async-done(((bf16[8,2,208,128]{3,2,1,0:T(8,128)(2,1)}), bf16[8,2,208,128]{3,2,1,0:T(8,128)(2,1)S(1)}, u32[]{:S(2)}, u32[]{:S(2)}) %all-to-all-start) | async-done | bytes 852000 | tf_op jit(solution)/shard_map/all_to_all | solution.py:396
  47.5 4.3 %all-to-all-start.1 = ((bf16[4,2,16,10368]{3,2,1,0:T(8,128)(2,1)}), bf16[4,2,16,10368]{3,2,1,0:T(8,128)(2,1)S(1)}, u32[]{:S(2)}, u32[]{:S(2)}) async-start(bf16[4,2,16,10368]{3,2,1,0:T(8,128)(2,1)} %copy_bitcast_fusion), calls=%async_computation.1 | async-start | bytes 5308416 | tf_op jit(solution)/shard_map/all_to_all | solution.py:366
  51.8 2.8 %collective-permute-start.12 = (bf16[4,2,144,128]{3,2,1,0:T(8,128)(2,1)}, bf16[4,2,144,128]{3,2,1,0:T(8,128)(2,1)S(1)}, u32[]{:S(2)}, u32[]{:S(2)}) collective-permute-start(bf16[4,2,144,128]{3,2,1,0:T(8,128)(2,1)} %collective-permute-done.11.refs_11_), channel_id=1, source_target_pairs={{0,8},{8,16},{16,24},{24,32},{32,40},{40,48},{48,56},{56,0},{1,9},... | collective-permute-start | bytes 884744 | tf_op jit(solution)/shard_map/ppermute | solution.py:382
  54.6 2.2 %collective-permute-start.2 = (bf16[8,2,208,128]{3,2,1,0:T(8,128)(2,1)S(1)}, bf16[8,2,208,128]{3,2,1,0:T(8,128)(2,1)}, u32[]{:S(2)}, u32[]{:S(2)}) collective-permute-start(bf16[8,2,208,128]{3,2,1,0:T(8,128)(2,1)S(1)} %all-to-all-done.refs_0_), channel_id=1, source_target_pairs={{0,64},{64,128},{128,192},{192,0},{1,65},{65,129},{129,193},{193,1... | collective-permute-start | bytes 2555912 | tf_op jit(solution)/shard_map/ppermute | solution.py:382
  57.4 1.3 collective-permute-start.1
  58.7 1.4 collective-permute-done.12.refs_10_
  60.0 1.5 collective-permute-start.13
  61.6 4.9 %collective-permute-done.10.refs_8_ = bf16[4,2,144,128]{3,2,1,0:T(8,128)(2,1)S(1)} collective-permute-done((bf16[4,2,144,128]{3,2,1,0:T(8,128)(2,1)}, bf16[4,2,144,128]{3,2,1,0:T(8,128)(2,1)S(1)}, u32[]{:S(2)}, u32[]{:S(2)}) %collective-permute-start.10) | collective-permute-done | bytes 294944 | tf_op jit(solution)/shard_map/ppermute | solution.py:387
  66.5 2.2 %collective-permute-done.13.refs_9_ = bf16[4,2,144,128]{3,2,1,0:T(8,128)(2,1)S(1)} collective-permute-done((bf16[4,2,144,128]{3,2,1,0:T(8,128)(2,1)S(1)}, bf16[4,2,144,128]{3,2,1,0:T(8,128)(2,1)S(1)}, u32[]{:S(2)}, u32[]{:S(2)}) %collective-permute-start.13) | collective-permute-done | bytes 294944 | tf_op jit(solution)/shard_map/ppermute | solution.py:382
  68.7 2.1 %collective-permute-start.14 = (bf16[4,2,80,128]{3,2,1,0:T(8,128)(2,1)S(1)}, bf16[4,2,80,128]{3,2,1,0:T(8,128)(2,1)S(1)}, u32[]{:S(2)}, u32[]{:S(2)}) collective-permute-start(bf16[4,2,80,128]{3,2,1,0:T(8,128)(2,1)S(1)} %slice.56), channel_id=1, source_target_pairs={{0,8},{8,16},{16,24},{24,32},{32,40},{40,48},{48,56},{56,0},{1,9},... | collective-permute-start | bytes 491528 | tf_op jit(solution)/shard_map/ppermute | solution.py:382
  70.8 2.8 %collective-permute-done.15.refs_13_ = bf16[4,2,64,128]{3,2,1,0:T(8,128)(2,1)S(1)} collective-permute-done((bf16[4,2,64,128]{3,2,1,0:T(8,128)(2,1)S(1)}, bf16[4,2,64,128]{3,2,1,0:T(8,128)(2,1)S(1)}, u32[]{:S(2)}, u32[]{:S(2)}) %collective-permute-start.15) | collective-permute-done | bytes 131104 | tf_op jit(solution)/shard_map/ppermute | solution.py:387
  73.6 2.3 %collective-permute-done.14.refs_12_ = bf16[4,2,80,128]{3,2,1,0:T(8,128)(2,1)S(1)} collective-permute-done((bf16[4,2,80,128]{3,2,1,0:T(8,128)(2,1)S(1)}, bf16[4,2,80,128]{3,2,1,0:T(8,128)(2,1)S(1)}, u32[]{:S(2)}, u32[]{:S(2)}) %collective-permute-start.14) | collective-permute-done | bytes 163872 | tf_op jit(solution)/shard_map/ppermute | solution.py:382
  77.6 3.9 %collective-permute-start.3 = (bf16[8,2,112,128]{3,2,1,0:T(8,128)(2,1)S(1)}, bf16[8,2,112,128]{3,2,1,0:T(8,128)(2,1)}, u32[]{:S(2)}, u32[]{:S(2)}) collective-permute-start(bf16[8,2,112,128]{3,2,1,0:T(8,128)(2,1)S(1)} %slice.54), channel_id=1, source_target_pairs={{0,64},{64,128},{128,192},{192,0},{1,65},{65,129},{129,193},{193,1... | collective-permute-start | bytes 1376264 | tf_op jit(solution)/shard_map/ppermute | solution.py:382
  84.0 1.5 collective-permute-start.4
  85.4 8.3 %collective-permute-done.3.refs_3_ = bf16[8,2,112,128]{3,2,1,0:T(8,128)(2,1)} collective-permute-done((bf16[8,2,112,128]{3,2,1,0:T(8,128)(2,1)S(1)}, bf16[8,2,112,128]{3,2,1,0:T(8,128)(2,1)}, u32[]{:S(2)}, u32[]{:S(2)}) %collective-permute-start.3) | collective-permute-done | bytes 458784 | tf_op jit(solution)/shard_map/ppermute | solution.py:382
  93.7 1.4 collective-permute-done.4.refs_4_
  95.4 2.0 %collective-permute-done.20.refs_18_ = bf16[8,2,96,128]{3,2,1,0:T(8,128)(2,1)} collective-permute-done((bf16[8,2,96,128]{3,2,1,0:T(8,128)(2,1)}, bf16[8,2,96,128]{3,2,1,0:T(8,128)(2,1)}, u32[]{:S(2)}, u32[]{:S(2)}) %collective-permute-start.20) | collective-permute-done | bytes 393248 | tf_op jit(solution)/shard_map/ppermute | solution.py:391
  97.4 40.2 %rows_work.1 = bf16[4,1312,128]{2,1,0:T(8,128)(2,1)} custom-call(s32[128]{0:T(128)} %order_ref.3, bf16[8,2,208,128]{3,2,1,0:T(8,128)(2,1)} %copy-done.1, bf16[8,2,208,128]{3,2,1,0:T(8,128)(2,1)} %collective-permute-done.1.refs_1_, bf16[8,2,208,128]{3,2,1,0:T(8,128)(2,1)} %collective-permute-done.2.refs_2_, ...), custom_call_target="tpu_custom_call" | custom-call | tf_op jit(solution)/shard_map/rows_work/pallas_call | solution.py:298
  137.6 23.3 %all_to_all.20.got_ref = bf16[4,1312,128]{2,1,0:T(8,128)(2,1)} all-to-all(bf16[4,1312,128]{2,1,0:T(8,128)(2,1)} %rows_work.1), channel_id=1, replica_groups=mesh['ctx_0'=4,'ctx_1'=8,'ctx_2'=2,'head'=4] {'head'}, dimensions={0} | all-to-all | bytes 2686976 | tf_op jit(solution)/shard_map/all_to_all | solution.py:369
  160.9 2.6 %spread_keys.1 = bf16[64,32,128]{2,1,0:T(8,128)(2,1)} custom-call(s32[128]{0:T(128)} %order_ref.3, bf16[4,1312,128]{2,1,0:T(8,128)(2,1)} %all_to_all.20.got_ref), custom_call_target="tpu_custom_call" | custom-call | tf_op jit(solution)/shard_map/spread_keys/pallas_call | solution.py:346
  163.4 7.4 %all-to-all-start.3 = ((bf16[64,32,128]{2,1,0:T(8,128)(2,1)}), bf16[64,32,128]{2,1,0:T(8,128)(2,1)S(1)}, u32[]{:S(2)}, u32[]{:S(2)}) async-start(bf16[64,32,128]{2,1,0:T(8,128)(2,1)} %spread_keys.1), calls=%async_computation.3 | async-start | bytes 1048576 | tf_op jit(solution)/shard_map/all_to_all | solution.py:370
  173.1 14.4 %all-to-all-done.3 = bf16[64,32,128]{2,1,0:T(8,128)(2,1)S(1)} async-done(((bf16[64,32,128]{2,1,0:T(8,128)(2,1)}), bf16[64,32,128]{2,1,0:T(8,128)(2,1)S(1)}, u32[]{:S(2)}, u32[]{:S(2)}) %all-to-all-start.3) | async-done | bytes 524320 | tf_op jit(solution)/shard_map/all_to_all | solution.py:370
  (92 shorter events, 12.3 us)
Async XLA Ops:
  3.2 4.9 %collective-permute-start.5 = (bf16[2,144,128]{2,1,0:T(8,128)(2,1)S(1)}, bf16[2,144,128]{2,1,0:T(8,128)(2,1)S(1)}, u32[]{:S(2)}, u32[]{:S(2)}) collective-permute-start(bf16[2,144,128]{2,1,0:T(8,128)(2,1)S(1)} %pad_maximum_fusion.3), channel_id=1, source_target_pairs={{0,192},{64,0},{128,64},{192,128},{1,193},{65,1},{129,65},{193,129... | collective-permute-start | bytes 221192 | tf_op jit(solution)/shard_map/ppermute | solution.py:387
  5.3 5.9 %collective-permute-start.6 = (bf16[2,144,128]{2,1,0:T(8,128)(2,1)S(1)}, bf16[2,144,128]{2,1,0:T(8,128)(2,1)S(1)}, u32[]{:S(2)}, u32[]{:S(2)}) collective-permute-start(bf16[2,144,128]{2,1,0:T(8,128)(2,1)S(1)} %pad_maximum_fusion.3), channel_id=1, source_target_pairs={{0,128},{64,192},{128,0},{192,64},{1,129},{65,193},{129,1},{193,65... | collective-permute-start | bytes 221192 | tf_op jit(solution)/shard_map/ppermute | solution.py:410
  6.2 5.0 %collective-permute-start.7 = (bf16[2,144,128]{2,1,0:T(8,128)(2,1)S(1)}, bf16[2,144,128]{2,1,0:T(8,128)(2,1)S(1)}, u32[]{:S(2)}, u32[]{:S(2)}) collective-permute-start(bf16[2,144,128]{2,1,0:T(8,128)(2,1)S(1)} %pad_maximum_fusion.3), channel_id=1, source_target_pairs={{0,64},{64,128},{128,192},{192,0},{1,65},{65,129},{129,193},{193,1... | collective-permute-start | bytes 221192 | tf_op jit(solution)/shard_map/ppermute | solution.py:382
  11.9 13.8 %collective-permute-start.11 = (bf16[4,2,144,128]{3,2,1,0:T(8,128)(2,1)}, bf16[4,2,144,128]{3,2,1,0:T(8,128)(2,1)}, u32[]{:S(2)}, u32[]{:S(2)}) collective-permute-start(bf16[4,2,144,128]{3,2,1,0:T(8,128)(2,1)} %pad_maximum_fusion.1.refs_5_), channel_id=1, source_target_pairs={{0,8},{8,16},{16,24},{24,32},{32,40},{40,48},{48,56},{56,0},{1,9},... | collective-permute-start | bytes 884744 | tf_op jit(solution)/shard_map/ppermute | solution.py:382
  13.5 12.7 %collective-permute-start.8 = (bf16[4,2,144,128]{3,2,1,0:T(8,128)(2,1)}, bf16[4,2,144,128]{3,2,1,0:T(8,128)(2,1)}, u32[]{:S(2)}, u32[]{:S(2)}) collective-permute-start(bf16[4,2,144,128]{3,2,1,0:T(8,128)(2,1)} %pad_maximum_fusion.1.refs_5_), channel_id=1, source_target_pairs={{0,56},{8,0},{16,8},{24,16},{32,24},{40,32},{48,40},{56,48},{1,57}... | collective-permute-start | bytes 884744 | tf_op jit(solution)/shard_map/ppermute | solution.py:387
  18.5 29.0 %all-to-all-start = ((bf16[8,2,208,128]{3,2,1,0:T(8,128)(2,1)}), bf16[8,2,208,128]{3,2,1,0:T(8,128)(2,1)S(1)}, u32[]{:S(2)}, u32[]{:S(2)}) async-start(bf16[8,2,208,128]{3,2,1,0:T(8,128)(2,1)} %broadcast_in_dim.3), calls=%async_computation | async-start | bytes 1703936 | tf_op jit(solution)/shard_map/all_to_all | solution.py:396
  25.6 31.2 %collective-permute-start.21 = (bf16[4,2,144,128]{3,2,1,0:T(8,128)(2,1)}, bf16[4,2,144,128]{3,2,1,0:T(8,128)(2,1)}, u32[]{:S(2)}, u32[]{:S(2)}) collective-permute-start(bf16[4,2,144,128]{3,2,1,0:T(8,128)(2,1)} %pad_maximum_fusion.1.refs_5_), channel_id=1, source_target_pairs={{0,4},{4,0},{1,5},{5,1},{2,6},{6,2},{3,7},{7,3},{8,12},{12,8},{9,1... | collective-permute-start | bytes 884744 | tf_op jit(solution)/shard_map/ppermute | solution.py:391
  25.7 31.7 %collective-permute-start.27 = (bf16[4,2,144,128]{3,2,1,0:T(8,128)(2,1)}, bf16[4,2,144,128]{3,2,1,0:T(8,128)(2,1)}, u32[]{:S(2)}, u32[]{:S(2)}) collective-permute-start(bf16[4,2,144,128]{3,2,1,0:T(8,128)(2,1)} %collective-permute-done.11.refs_11_), channel_id=1, source_target_pairs={{0,4},{4,0},{1,5},{5,1},{2,6},{6,2},{3,7},{7,3},{8,12},{12,8},{9,1... | collective-permute-start | bytes 884744 | tf_op jit(solution)/shard_map/ppermute | solution.py:391
  26.2 30.7 %collective-permute-start.9 = (bf16[4,2,144,128]{3,2,1,0:T(8,128)(2,1)}, bf16[4,2,144,128]{3,2,1,0:T(8,128)(2,1)}, u32[]{:S(2)}, u32[]{:S(2)}) collective-permute-start(bf16[4,2,144,128]{3,2,1,0:T(8,128)(2,1)} %collective-permute-done.8.refs_6_), channel_id=1, source_target_pairs={{0,56},{8,0},{16,8},{24,16},{32,24},{40,32},{48,40},{56,48},{1,57}... | collective-permute-start | bytes 884744 | tf_op jit(solution)/shard_map/ppermute | solution.py:387
  47.5 47.8 %all-to-all-start.1 = ((bf16[4,2,16,10368]{3,2,1,0:T(8,128)(2,1)}), bf16[4,2,16,10368]{3,2,1,0:T(8,128)(2,1)S(1)}, u32[]{:S(2)}, u32[]{:S(2)}) async-start(bf16[4,2,16,10368]{3,2,1,0:T(8,128)(2,1)} %copy_bitcast_fusion), calls=%async_computation.1 | async-start | bytes 5308416 | tf_op jit(solution)/shard_map/all_to_all | solution.py:366
  51.8 8.2 %collective-permute-start.12 = (bf16[4,2,144,128]{3,2,1,0:T(8,128)(2,1)}, bf16[4,2,144,128]{3,2,1,0:T(8,128)(2,1)S(1)}, u32[]{:S(2)}, u32[]{:S(2)}) collective-permute-start(bf16[4,2,144,128]{3,2,1,0:T(8,128)(2,1)} %collective-permute-done.11.refs_11_), channel_id=1, source_target_pairs={{0,8},{8,16},{16,24},{24,32},{32,40},{40,48},{48,56},{56,0},{1,9},... | collective-permute-start | bytes 884744 | tf_op jit(solution)/shard_map/ppermute | solution.py:382
  54.6 21.3 %collective-permute-start.2 = (bf16[8,2,208,128]{3,2,1,0:T(8,128)(2,1)S(1)}, bf16[8,2,208,128]{3,2,1,0:T(8,128)(2,1)}, u32[]{:S(2)}, u32[]{:S(2)}) collective-permute-start(bf16[8,2,208,128]{3,2,1,0:T(8,128)(2,1)S(1)} %all-to-all-done.refs_0_), channel_id=1, source_target_pairs={{0,64},{64,128},{128,192},{192,0},{1,65},{65,129},{129,193},{193,1... | collective-permute-start | bytes 2555912 | tf_op jit(solution)/shard_map/ppermute | solution.py:382
  56.8 4.8 %collective-permute-start.22 = (bf16[4,2,144,128]{3,2,1,0:T(8,128)(2,1)}, bf16[4,2,144,128]{3,2,1,0:T(8,128)(2,1)S(1)}, u32[]{:S(2)}, u32[]{:S(2)}) collective-permute-start(bf16[4,2,144,128]{3,2,1,0:T(8,128)(2,1)} %collective-permute-done.8.refs_6_), channel_id=1, source_target_pairs={{0,4},{4,0},{1,5},{5,1},{2,6},{6,2},{3,7},{7,3},{8,12},{12,8},{9,1... | collective-permute-start | bytes 884744 | tf_op jit(solution)/shard_map/ppermute | solution.py:391
  56.8 9.6 %collective-permute-start.10 = (bf16[4,2,144,128]{3,2,1,0:T(8,128)(2,1)}, bf16[4,2,144,128]{3,2,1,0:T(8,128)(2,1)S(1)}, u32[]{:S(2)}, u32[]{:S(2)}) collective-permute-start(bf16[4,2,144,128]{3,2,1,0:T(8,128)(2,1)} %collective-permute-done.9.refs_7_), channel_id=1, source_target_pairs={{0,56},{8,0},{16,8},{24,16},{32,24},{40,32},{48,40},{56,48},{1,57}... | collective-permute-start | bytes 884744 | tf_op jit(solution)/shard_map/ppermute | solution.py:387
  57.4 24.8 %collective-permute-start.1 = (bf16[8,2,208,128]{3,2,1,0:T(8,128)(2,1)S(1)}, bf16[8,2,208,128]{3,2,1,0:T(8,128)(2,1)}, u32[]{:S(2)}, u32[]{:S(2)}) collective-permute-start(bf16[8,2,208,128]{3,2,1,0:T(8,128)(2,1)S(1)} %all-to-all-done.refs_0_), channel_id=1, source_target_pairs={{0,192},{64,0},{128,64},{192,128},{1,193},{65,1},{129,65},{193,129... | collective-permute-start | bytes 2555912 | tf_op jit(solution)/shard_map/ppermute | solution.py:387
  60.0 8.6 %collective-permute-start.13 = (bf16[4,2,144,128]{3,2,1,0:T(8,128)(2,1)S(1)}, bf16[4,2,144,128]{3,2,1,0:T(8,128)(2,1)S(1)}, u32[]{:S(2)}, u32[]{:S(2)}) collective-permute-start(bf16[4,2,144,128]{3,2,1,0:T(8,128)(2,1)S(1)} %collective-permute-done.12.refs_10_), channel_id=1, source_target_pairs={{0,8},{8,16},{16,24},{24,32},{32,40},{40,48},{48,56},{56,0},{1,9},... | collective-permute-start | bytes 884744 | tf_op jit(solution)/shard_map/ppermute | solution.py:382
  61.6 7.1 %collective-permute-start.26 = (bf16[4,2,144,128]{3,2,1,0:T(8,128)(2,1)S(1)}, bf16[4,2,144,128]{3,2,1,0:T(8,128)(2,1)S(1)}, u32[]{:S(2)}, u32[]{:S(2)}) collective-permute-start(bf16[4,2,144,128]{3,2,1,0:T(8,128)(2,1)S(1)} %collective-permute-done.12.refs_10_), channel_id=1, source_target_pairs={{0,4},{4,0},{1,5},{5,1},{2,6},{6,2},{3,7},{7,3},{8,12},{12,8},{9,1... | collective-permute-start | bytes 884744 | tf_op jit(solution)/shard_map/ppermute | solution.py:391
  66.5 4.3 %collective-permute-start.23 = (bf16[4,2,144,128]{3,2,1,0:T(8,128)(2,1)}, bf16[4,2,144,128]{3,2,1,0:T(8,128)(2,1)S(1)}, u32[]{:S(2)}, u32[]{:S(2)}) collective-permute-start(bf16[4,2,144,128]{3,2,1,0:T(8,128)(2,1)} %collective-permute-done.9.refs_7_), channel_id=1, source_target_pairs={{0,4},{4,0},{1,5},{5,1},{2,6},{6,2},{3,7},{7,3},{8,12},{12,8},{9,1... | collective-permute-start | bytes 884744 | tf_op jit(solution)/shard_map/ppermute | solution.py:391
  68.7 5.0 %collective-permute-start.15 = (bf16[4,2,64,128]{3,2,1,0:T(8,128)(2,1)S(1)}, bf16[4,2,64,128]{3,2,1,0:T(8,128)(2,1)S(1)}, u32[]{:S(2)}, u32[]{:S(2)}) collective-permute-start(bf16[4,2,64,128]{3,2,1,0:T(8,128)(2,1)S(1)} %slice.57), channel_id=1, source_target_pairs={{0,56},{8,0},{16,8},{24,16},{32,24},{40,32},{48,40},{56,48},{1,57}... | collective-permute-start | bytes 393224 | tf_op jit(solution)/shard_map/ppermute | solution.py:387
  68.7 7.2 %collective-permute-start.14 = (bf16[4,2,80,128]{3,2,1,0:T(8,128)(2,1)S(1)}, bf16[4,2,80,128]{3,2,1,0:T(8,128)(2,1)S(1)}, u32[]{:S(2)}, u32[]{:S(2)}) collective-permute-start(bf16[4,2,80,128]{3,2,1,0:T(8,128)(2,1)S(1)} %slice.56), channel_id=1, source_target_pairs={{0,8},{8,16},{16,24},{24,32},{32,40},{40,48},{48,56},{56,0},{1,9},... | collective-permute-start | bytes 491528 | tf_op jit(solution)/shard_map/ppermute | solution.py:382
  70.8 10.8 %collective-permute-start.25 = (bf16[4,2,144,128]{3,2,1,0:T(8,128)(2,1)S(1)}, bf16[4,2,144,128]{3,2,1,0:T(8,128)(2,1)S(1)}, u32[]{:S(2)}, u32[]{:S(2)}) collective-permute-start(bf16[4,2,144,128]{3,2,1,0:T(8,128)(2,1)S(1)} %collective-permute-done.13.refs_9_), channel_id=1, source_target_pairs={{0,4},{4,0},{1,5},{5,1},{2,6},{6,2},{3,7},{7,3},{8,12},{12,8},{9,1... | collective-permute-start | bytes 884744 | tf_op jit(solution)/shard_map/ppermute | solution.py:391
  73.6 8.1 %collective-permute-start.24 = (bf16[4,2,144,128]{3,2,1,0:T(8,128)(2,1)S(1)}, bf16[4,2,144,128]{3,2,1,0:T(8,128)(2,1)S(1)}, u32[]{:S(2)}, u32[]{:S(2)}) collective-permute-start(bf16[4,2,144,128]{3,2,1,0:T(8,128)(2,1)S(1)} %collective-permute-done.10.refs_8_), channel_id=1, source_target_pairs={{0,4},{4,0},{1,5},{5,1},{2,6},{6,2},{3,7},{7,3},{8,12},{12,8},{9,1... | collective-permute-start | bytes 884744 | tf_op jit(solution)/shard_map/ppermute | solution.py:391
  75.9 1.7 collective-permute-start.29
  76.0 8.0 %collective-permute-start.28 = (bf16[4,2,80,128]{3,2,1,0:T(8,128)(2,1)S(1)}, bf16[4,2,80,128]{3,2,1,0:T(8,128)(2,1)S(1)}, u32[]{:S(2)}, u32[]{:S(2)}) collective-permute-start(bf16[4,2,80,128]{3,2,1,0:T(8,128)(2,1)S(1)} %collective-permute-done.14.refs_12_), channel_id=1, source_target_pairs={{0,4},{4,0},{1,5},{5,1},{2,6},{6,2},{3,7},{7,3},{8,12},{12,8},{9,1... | collective-permute-start | bytes 491528 | tf_op jit(solution)/shard_map/ppermute | solution.py:391
  77.6 16.1 %collective-permute-start.3 = (bf16[8,2,112,128]{3,2,1,0:T(8,128)(2,1)S(1)}, bf16[8,2,112,128]{3,2,1,0:T(8,128)(2,1)}, u32[]{:S(2)}, u32[]{:S(2)}) collective-permute-start(bf16[8,2,112,128]{3,2,1,0:T(8,128)(2,1)S(1)} %slice.54), channel_id=1, source_target_pairs={{0,64},{64,128},{128,192},{192,0},{1,65},{65,129},{129,193},{193,1... | collective-permute-start | bytes 1376264 | tf_op jit(solution)/shard_map/ppermute | solution.py:382
  81.6 13.8 %collective-permute-start.16 = (bf16[8,2,208,128]{3,2,1,0:T(8,128)(2,1)S(1)}, bf16[8,2,208,128]{3,2,1,0:T(8,128)(2,1)}, u32[]{:S(2)}, u32[]{:S(2)}) collective-permute-start(bf16[8,2,208,128]{3,2,1,0:T(8,128)(2,1)S(1)} %all-to-all-done.refs_0_), channel_id=1, source_target_pairs={{0,4},{4,0},{1,5},{5,1},{2,6},{6,2},{3,7},{7,3},{8,12},{12,8},{9,1... | collective-permute-start | bytes 2555912 | tf_op jit(solution)/shard_map/ppermute | solution.py:391
  81.7 15.7 %collective-permute-start.18 = (bf16[8,2,208,128]{3,2,1,0:T(8,128)(2,1)}, bf16[8,2,208,128]{3,2,1,0:T(8,128)(2,1)}, u32[]{:S(2)}, u32[]{:S(2)}) collective-permute-start(bf16[8,2,208,128]{3,2,1,0:T(8,128)(2,1)} %collective-permute-done.2.refs_2_), channel_id=1, source_target_pairs={{0,4},{4,0},{1,5},{5,1},{2,6},{6,2},{3,7},{7,3},{8,12},{12,8},{9,1... | collective-permute-start | bytes 2555912 | tf_op jit(solution)/shard_map/ppermute | solution.py:391
  82.4 15.0 %collective-permute-start.17 = (bf16[8,2,208,128]{3,2,1,0:T(8,128)(2,1)}, bf16[8,2,208,128]{3,2,1,0:T(8,128)(2,1)}, u32[]{:S(2)}, u32[]{:S(2)}) collective-permute-start(bf16[8,2,208,128]{3,2,1,0:T(8,128)(2,1)} %collective-permute-done.1.refs_1_), channel_id=1, source_target_pairs={{0,4},{4,0},{1,5},{5,1},{2,6},{6,2},{3,7},{7,3},{8,12},{12,8},{9,1... | collective-permute-start | bytes 2555912 | tf_op jit(solution)/shard_map/ppermute | solution.py:391
  84.0 11.2 %collective-permute-start.4 = (bf16[8,2,96,128]{3,2,1,0:T(8,128)(2,1)S(1)}, bf16[8,2,96,128]{3,2,1,0:T(8,128)(2,1)}, u32[]{:S(2)}, u32[]{:S(2)}) collective-permute-start(bf16[8,2,96,128]{3,2,1,0:T(8,128)(2,1)S(1)} %slice.55), channel_id=1, source_target_pairs={{0,192},{64,0},{128,64},{192,128},{1,193},{65,1},{129,65},{193,129... | collective-permute-start | bytes 1179656 | tf_op jit(solution)/shard_map/ppermute | solution.py:387
  93.7 3.6 %collective-permute-start.19 = (bf16[8,2,112,128]{3,2,1,0:T(8,128)(2,1)}, bf16[8,2,112,128]{3,2,1,0:T(8,128)(2,1)}, u32[]{:S(2)}, u32[]{:S(2)}) collective-permute-start(bf16[8,2,112,128]{3,2,1,0:T(8,128)(2,1)} %collective-permute-done.3.refs_3_), channel_id=1, source_target_pairs={{0,4},{4,0},{1,5},{5,1},{2,6},{6,2},{3,7},{7,3},{8,12},{12,8},{9,1... | collective-permute-start | bytes 1376264 | tf_op jit(solution)/shard_map/ppermute | solution.py:391
  95.2 2.2 %collective-permute-start.20 = (bf16[8,2,96,128]{3,2,1,0:T(8,128)(2,1)}, bf16[8,2,96,128]{3,2,1,0:T(8,128)(2,1)}, u32[]{:S(2)}, u32[]{:S(2)}) collective-permute-start(bf16[8,2,96,128]{3,2,1,0:T(8,128)(2,1)} %collective-permute-done.4.refs_4_), channel_id=1, source_target_pairs={{0,4},{4,0},{1,5},{5,1},{2,6},{6,2},{3,7},{7,3},{8,12},{12,8},{9,1... | collective-permute-start | bytes 1179656 | tf_op jit(solution)/shard_map/ppermute | solution.py:391
  163.4 24.1 %all-to-all-start.3 = ((bf16[64,32,128]{2,1,0:T(8,128)(2,1)}), bf16[64,32,128]{2,1,0:T(8,128)(2,1)S(1)}, u32[]{:S(2)}, u32[]{:S(2)}) async-start(bf16[64,32,128]{2,1,0:T(8,128)(2,1)} %spread_keys.1), calls=%async_computation.3 | async-start | bytes 1048576 | tf_op jit(solution)/shard_map/all_to_all | solution.py:370
  (18 other events, 269.1 us)
where the time goes:
time: 190 us; the launch traced here: 188 us
  waiting for transfers between devices  60.5 us (32%)
  starting transfers between devices  49.6 us (26%)
  Pallas kernels  42.7 us (22%)
  blocking collectives  23.3 us (12%)
  local copies, waits for them, and re-layouts  6.2 us (3%)
  other arithmetic  4.95 us (3%)
    pallas_call x1, Pallas kernels, rows_call(): pl.pallas_call(rows_kernel, out_shape=jax.ShapeDtypeStruct((HEADS, KEY_RO...  40.2 us
    all_to_all x1, blocking collectives, work(): got = lax.all_to_all(sent, 'head', split_axis=0, concat_axis=0, tiled=True)  23.3 us
    all_to_all x1, waiting for transfers between devices, sent_to_all(): return lax.all_to_all(copies, axis, split_axis=0, concat_axis=0, tiled=True)  16.4 us
    ppermute x7, starting transfers between devices, onward(): return lax.ppermute(piece, axis, [(i, (i + 1) % n) for i in range(n)])  16.1 us
    all_to_all x1, waiting for transfers between devices, work(): lax.all_to_all(spread_call(block_order, got), CTX, split_axis=0, concat_a...  14.4 us
    ppermute x7, waiting for transfers between devices, onward(): return lax.ppermute(piece, axis, [(i, (i + 1) % n) for i in range(n)])  14.2 us
    ppermute x7, starting transfers between devices, backward(): return lax.ppermute(piece, axis, [(i, (i - 1) % n) for i in range(n)])  12.6 us
    ppermute x7, waiting for transfers between devices, backward(): return lax.ppermute(piece, axis, [(i, (i - 1) % n) for i in range(n)])  9.14 us
  transfers between devices with their start and end apart: 33, of which 12 were waited for; matrix products, arithmetic and copies ran while one was open for 4% of the time, Pallas kernels for 0%

commit v1 on v0

--- a/solution.py
+++ b/solution.py
@@ -32,10 +32,10 @@
 KEY_ROWS = 1024
 GRAD_ROWS = 9 * 2 * GROUP
 HALF_ROWS = (KW + DI) // 2
-STRIP = 208
-STRIP_CUT = 112
+STRIP = 176
+STRIP_CUT = 96
 REST = HALF_ROWS - STRIP
-REST_CUT = 80
+REST_CUT = 96
 PIECES = 14
 masked_value = -1e30
 SCORE_EXP2 = math.log2(math.e) / math.sqrt(HEAD_QK)
@@ -100,8 +100,8 @@
     def arrived(n):
         pltpu.make_async_copy(raw.at[n], raw.at[n], sems.at[n]).wait()
 
-    keys[0:64, :] = jnp.zeros((64, LENGTH), bf16)
-    keys[640:704, :] = jnp.zeros((64, LENGTH), bf16)
+    keys[:, 0:64, :] = jnp.zeros((LENGTH // WIDE, 64, WIDE), bf16)
+    keys[:, 640:704, :] = jnp.zeros((LENGTH // WIDE, 64, WIDE), bf16)
 
     for e in range(2):
         for src in range(HEADS):
@@ -126,12 +126,11 @@
         arrived(2 * i + 1)
         both = jnp.concatenate([raw[2 * i], raw[2 * i + 1]], axis=1)
         mixed = jnp.dot(both, shuffle, preferred_element_type=f32).astype(bf16)
-        early = pl.multiple_of(i * 128, 128)
-        late = pl.multiple_of(HALF + i * 128, 128)
-        keys[64:640, pl.ds(early, 128)] = mixed[0:KW, 0:128]
-        keys[704:832, pl.ds(early, 128)] = mixed[KW:, 0:128]
-        keys[64:640, pl.ds(late, 128)] = mixed[0:KW, 128:256]
-        keys[704:832, pl.ds(late, 128)] = mixed[KW:, 128:256]
+        for late in range(2):
+            n = late * (HALF // WIDE) + i // 4
+            lanes = pl.ds(pl.multiple_of(i % 4 * 128, 128), 128)
+            keys[n, 64:640, lanes] = mixed[0:KW, late * 128 : late * 128 + 128]
+            keys[n, 704:832, lanes] = mixed[KW:, late * 128 : late * 128 + 128]
         return carry
 
     lax.fori_loop(0, 16, sort_pair, 0)
@@ -170,12 +169,13 @@
             at = pl.multiple_of(at * WIDE, WIDE)
             visible = key_pos(at, WIDE) <= row_pos
             for parity in range(2):
-                k = keys[64 * (1 - parity) : 64 * (1 - parity) + 640, pl.ds(at, WIDE)]
+                k = keys[at // WIDE, 64 * (1 - parity) : 64 * (1 - parity) + 640, :]
                 s = jnp.dot(q_all[e, parity], k, preferred_element_type=f32)
                 s = jnp.where(visible[None], s.reshape(HM // 2, GROUP, WIDE), masked_value)
                 s = s.reshape(ROWS // 2, WIDE)
                 r = slice(parity * (ROWS // 2), (parity + 1) * (ROWS // 2))
-                scores[r, pl.ds(at, WIDE)] = s
+                for i in range(WIDE // 128):
+                    scores[at // 128 + i, r] = s[:, i * 128 : (i + 1) * 128]
                 top = jnp.maximum(s[:, 0:128], s[:, 128:256])
                 best[r] = jnp.maximum(best[r], jnp.maximum(top, jnp.maximum(s[:, 256:384], s[:, 384:512])))
             return carry
@@ -196,9 +196,9 @@
                 top = best[r]
                 part = total[r]
                 for half in range(TILE // 128):
-                    lanes = pl.ds(pl.multiple_of(at + half * 128, 128), 128)
-                    raised = jnp.exp2((scores[r, lanes] - top) * SCORE_EXP2)
-                    scores[r, lanes] = raised
+                    n = at // 128 + half
+                    raised = jnp.exp2((scores[n, r] - top) * SCORE_EXP2)
+                    scores[n, r] = raised
                     part = part + raised
                 total[r] = part
             return carry
@@ -215,7 +215,7 @@
 
         def index_logits(at):
             act = jnp.dot(
-                qi_all[e], keys[704:832, pl.ds(at, TILE)], preferred_element_type=f32
+                qi_all[e], keys[at // WIDE, 704:832, pl.ds(pl.multiple_of(at % WIDE, TILE), TILE)], preferred_element_type=f32
             )
             out = jnp.zeros((GROUP, TILE), f32)
             for h in range(HI):
@@ -227,12 +227,13 @@
         def target_step(j, carry):
             at = tile_at(j)
             lanes = pl.ds(at, TILE)
-            acc = jnp.zeros((GROUP, TILE), f32)
+            acc = [jnp.zeros((GROUP, 128), f32) for _ in range(TILE // 128)]
             for h in range(HM):
                 r = slice(h * GROUP, (h + 1) * GROUP)
                 share = total[r]
-                acc = acc + scores[r, lanes] * jnp.concatenate([share, share], axis=1)
-            target[:, lanes] = acc
+                for half in range(TILE // 128):
+                    acc[half] = acc[half] + scores[at // 128 + half, r] * share
+            target[:, lanes] = jnp.concatenate(acc, axis=1)
             visible = key_pos(at, TILE) <= row_pos
             logits[:, lanes] = jnp.where(visible, index_logits(at), masked_value)
             return carry
@@ -254,7 +255,7 @@
         def back_step(j, carry):
             at = j if e == 0 else jnp.where(j < HALF // WIDE, j, j + c_own // 8)
             lanes = pl.ds(pl.multiple_of(at * WIDE, WIDE), WIDE)
-            k = keys[704:832, lanes]
+            k = keys[at, 704:832, :]
             act = jnp.dot(qi_all[e], k, preferred_element_type=f32)
             through = jnp.where(
                 act.reshape(HI, GROUP, WIDE) > 0.0, slope[:, lanes][None], 0.0
@@ -306,10 +307,10 @@
         out_specs=pl.BlockSpec(memory_space=pltpu.VMEM),
         scratch_shapes=[
             pltpu.VMEM((32, KW + DI, 128), bf16),
-            pltpu.VMEM((832, LENGTH), bf16),
+            pltpu.VMEM((LENGTH // WIDE, 832, WIDE), bf16),
             pltpu.VMEM((2, 2, ROWS // 2, 640), bf16),
             pltpu.VMEM((2, IROWS, DI), bf16),
-            pltpu.VMEM((ROWS, LENGTH), f32),
+            pltpu.VMEM((LENGTH // 128, ROWS, 128), f32),
             pltpu.VMEM((ROWS, 128), f32),
             pltpu.VMEM((ROWS, 128), f32),
             pltpu.VMEM((2, IROWS, DI), f32),
@@ -412,8 +413,8 @@
     b1, f1 = backward(rows, z), onward(rows, z)
     down1, up1 = backward(planes, y), onward(planes, y)
     b2, f2 = backward(b1, z), onward(f1, z)
+    b3, f3 = backward(b2, z), onward(f2, z)
     up2, down2 = onward(up1[:, :, :STRIP_CUT], y), backward(down1[:, :, STRIP_CUT:], y)
-    b3, f3 = backward(b2, z), onward(f2, z)
     f4, b4 = onward(f3[:, :, :REST_CUT], z), backward(b3[:, :, REST_CUT:], z)
     own = [planes, down1, up1, up2, down2, rows, b1, b2, b3, f3, f2, f1, f4, b4]
     return own + [swapped(piece) for piece in own]

time: 190 us -> 188 us (0.989)
  waiting for transfers between devices: 60.5 us -> 64.7 us
  Pallas kernels: 42.7 us -> 38.8 us
  starting transfers between devices: 49.6 us -> 46.2 us
    ppermute x7, waiting for transfers between devices: 14.2 us -> 23.9 us  [onward(): return lax.ppermute(piece, axis, [(i, (i + 1) % n) for i in range(n)])]
    ppermute x7, starting transfers between devices: 16.1 us -> 9 us  [onward(): return lax.ppermute(piece, axis, [(i, (i + 1) % n) for i in range(n)])]
    pallas_call x1, Pallas kernels: 40.2 us -> 36.3 us  [rows_call(): pl.pallas_call(rows_kernel, out_shape=jax.ShapeDtypeStruct((HEADS, KEY_RO...]
    all_to_all x1, waiting for transfers between devices: 16.4 us -> 12.7 us  [sent_to_all(): return lax.all_to_all(copies, axis, split_axis=0, concat_axis=0, tiled=True)]
    all_to_all x1, starting transfers between devices: 7.4 us -> 9.86 us  [work(): lax.all_to_all(spread_call(block_order, got), CTX, split_axis=0, concat_a...]
    all_to_all x1, starting transfers between devices: 5.84 us -> 3.54 us  [sent_to_all(): return lax.all_to_all(copies, axis, split_axis=0, concat_axis=0, tiled=True)]
    ppermute x7, starting transfers between devices: 12.6 us -> 14.7 us  [backward(): return lax.ppermute(piece, axis, [(i, (i - 1) % n) for i in range(n)])]
  transfers between devices with their start and end apart: 33 -> 33, of which waited for: 12 -> 15; matrix products, arithmetic and copies ran while one was open for 4% -> 5% of each run, Pallas kernels for 0% -> 0%
where the time goes in v1:
time: 188 us; the launch traced here: 186 us
  waiting for transfers between devices  64.7 us (34%)
  starting transfers between devices  46.2 us (25%)
  Pallas kernels  38.8 us (21%)
  blocking collectives  23.2 us (12%)
  local copies, waits for them, and re-layouts  6.53 us (3%)
  other arithmetic  4.98 us (3%)
    pallas_call x1, Pallas kernels, rows_call(): pl.pallas_call(rows_kernel, out_shape=jax.ShapeDtypeStruct((HEADS, KEY_RO...  36.3 us
    ppermute x7, waiting for transfers between devices, onward(): return lax.ppermute(piece, axis, [(i, (i + 1) % n) for i in range(n)])  23.9 us
    all_to_all x1, blocking collectives, work(): got = lax.all_to_all(sent, 'head', split_axis=0, concat_axis=0, tiled=True)  23.2 us
    ppermute x7, starting transfers between devices, backward(): return lax.ppermute(piece, axis, [(i, (i - 1) % n) for i in range(n)])  14.7 us
    all_to_all x1, waiting for transfers between devices, work(): lax.all_to_all(spread_call(block_order, got), CTX, split_axis=0, concat_a...  14.4 us
    all_to_all x1, waiting for transfers between devices, sent_to_all(): return lax.all_to_all(copies, axis, split_axis=0, concat_axis=0, tiled=True)  12.7 us
    all_to_all x1, starting transfers between devices, work(): lax.all_to_all(spread_call(block_order, got), CTX, split_axis=0, concat_a...  9.86 us
    ppermute x7, starting transfers between devices, onward(): return lax.ppermute(piece, axis, [(i, (i + 1) % n) for i in range(n)])  9 us
  transfers between devices with their start and end apart: 33, of which 15 were waited for; matrix products, arithmetic and copies ran while one was open for 5% of the time, Pallas kernels for 0%

profile of v1, /device:TPU:8, one launch (start us, length us, event | category | flops | bytes accessed | tf_op | source)
XLA Modules:
  0.0 185.5 jit_solution(2040222533375109671)
XLA Ops:
  0.6 1.1 broadcast_select_fusion
  1.9 1.3 collective-permute-done
  3.2 2.4 %collective-permute-start.6 = (bf16[2,176,128]{2,1,0:T(8,128)(2,1)S(1)}, bf16[2,176,128]{2,1,0:T(8,128)(2,1)S(1)}, u32[]{:S(2)}, u32[]{:S(2)}) collective-permute-start(bf16[2,176,128]{2,1,0:T(8,128)(2,1)S(1)} %get-tuple-element.12), channel_id=1, source_target_pairs={{0,128},{64,192},{128,0},{192,64},{1,129},{65,193},{129,1},{193,65... | collective-permute-start | bytes 270344 | tf_op jit(solution)/shard_map/ppermute | solution.py:411
  5.5 1.3 collective-permute-start.5
  7.6 2.5 %collective-permute-done.6 = bf16[2,176,128]{2,1,0:T(8,128)(2,1)S(1)} collective-permute-done((bf16[2,176,128]{2,1,0:T(8,128)(2,1)S(1)}, bf16[2,176,128]{2,1,0:T(8,128)(2,1)S(1)}, u32[]{:S(2)}, u32[]{:S(2)}) %collective-permute-start.6) | collective-permute-done | bytes 90144 | tf_op jit(solution)/shard_map/ppermute | solution.py:411
  10.1 1.3 collective-permute-done.5
  12.2 5.9 %collective-permute-start.8 = (bf16[4,2,176,128]{3,2,1,0:T(8,128)(2,1)}, bf16[4,2,176,128]{3,2,1,0:T(8,128)(2,1)}, u32[]{:S(2)}, u32[]{:S(2)}) collective-permute-start(bf16[4,2,176,128]{3,2,1,0:T(8,128)(2,1)} %pad_maximum_fusion.1.refs_5_), channel_id=1, source_target_pairs={{0,56},{8,0},{16,8},{24,16},{32,24},{40,32},{48,40},{56,48},{1,57}... | collective-permute-start | bytes 1081352 | tf_op jit(solution)/shard_map/ppermute | solution.py:388
  18.9 1.1 concatenate.15
  21.0 3.5 %all-to-all-start = ((bf16[8,2,176,128]{3,2,1,0:T(8,128)(2,1)}), bf16[8,2,176,128]{3,2,1,0:T(8,128)(2,1)S(1)}, u32[]{:S(2)}, u32[]{:S(2)}) async-start(bf16[8,2,176,128]{3,2,1,0:T(8,128)(2,1)} %broadcast_in_dim.3), calls=%async_computation | async-start | bytes 1441792 | tf_op jit(solution)/shard_map/all_to_all | solution.py:397
  24.5 1.9 %collective-permute-start.11 = (bf16[4,2,176,128]{3,2,1,0:T(8,128)(2,1)}, bf16[4,2,176,128]{3,2,1,0:T(8,128)(2,1)}, u32[]{:S(2)}, u32[]{:S(2)}) collective-permute-start(bf16[4,2,176,128]{3,2,1,0:T(8,128)(2,1)} %pad_maximum_fusion.1.refs_5_), channel_id=1, source_target_pairs={{0,8},{8,16},{16,24},{24,32},{32,40},{40,48},{48,56},{56,0},{1,9},... | collective-permute-start | bytes 1081352 | tf_op jit(solution)/shard_map/ppermute | solution.py:383
  26.4 1.3 collective-permute-done.8.refs_6_
  27.7 3.9 %collective-permute-start.9 = (bf16[4,2,176,128]{3,2,1,0:T(8,128)(2,1)}, bf16[4,2,176,128]{3,2,1,0:T(8,128)(2,1)}, u32[]{:S(2)}, u32[]{:S(2)}) collective-permute-start(bf16[4,2,176,128]{3,2,1,0:T(8,128)(2,1)} %collective-permute-done.8.refs_6_), channel_id=1, source_target_pairs={{0,56},{8,0},{16,8},{24,16},{32,24},{40,32},{48,40},{56,48},{1,57}... | collective-permute-start | bytes 1081352 | tf_op jit(solution)/shard_map/ppermute | solution.py:388
  31.7 1.7 copy_bitcast_fusion
  33.4 12.7 %all-to-all-done.refs_0_ = bf16[8,2,176,128]{3,2,1,0:T(8,128)(2,1)S(1)} async-done(((bf16[8,2,176,128]{3,2,1,0:T(8,128)(2,1)}), bf16[8,2,176,128]{3,2,1,0:T(8,128)(2,1)S(1)}, u32[]{:S(2)}, u32[]{:S(2)}) %all-to-all-start) | async-done | bytes 720928 | tf_op jit(solution)/shard_map/all_to_all | solution.py:397
  46.0 4.3 %all-to-all-start.1 = ((bf16[4,2,16,10368]{3,2,1,0:T(8,128)(2,1)}), bf16[4,2,16,10368]{3,2,1,0:T(8,128)(2,1)S(1)}, u32[]{:S(2)}, u32[]{:S(2)}) async-start(bf16[4,2,16,10368]{3,2,1,0:T(8,128)(2,1)} %copy_bitcast_fusion), calls=%async_computation.1 | async-start | bytes 5308416 | tf_op jit(solution)/shard_map/all_to_all | solution.py:367
  51.2 1.1 collective-permute-start.12
  52.8 2.1 %collective-permute-start.10 = (bf16[4,2,176,128]{3,2,1,0:T(8,128)(2,1)}, bf16[4,2,176,128]{3,2,1,0:T(8,128)(2,1)S(1)}, u32[]{:S(2)}, u32[]{:S(2)}) collective-permute-start(bf16[4,2,176,128]{3,2,1,0:T(8,128)(2,1)} %collective-permute-done.9.refs_7_), channel_id=1, source_target_pairs={{0,56},{8,0},{16,8},{24,16},{32,24},{40,32},{48,40},{56,48},{1,57}... | collective-permute-start | bytes 1081352 | tf_op jit(solution)/shard_map/ppermute | solution.py:388
  55.0 7.1 %collective-permute-done.12.refs_10_ = bf16[4,2,176,128]{3,2,1,0:T(8,128)(2,1)S(1)} collective-permute-done((bf16[4,2,176,128]{3,2,1,0:T(8,128)(2,1)}, bf16[4,2,176,128]{3,2,1,0:T(8,128)(2,1)S(1)}, u32[]{:S(2)}, u32[]{:S(2)}) %collective-permute-start.12) | collective-permute-done | bytes 360480 | tf_op jit(solution)/shard_map/ppermute | solution.py:383
  62.1 1.6 collective-permute-start.2
  65.1 6.8 %collective-permute-done.13.refs_9_ = bf16[4,2,176,128]{3,2,1,0:T(8,128)(2,1)S(1)} collective-permute-done((bf16[4,2,176,128]{3,2,1,0:T(8,128)(2,1)S(1)}, bf16[4,2,176,128]{3,2,1,0:T(8,128)(2,1)S(1)}, u32[]{:S(2)}, u32[]{:S(2)}) %collective-permute-start.13) | collective-permute-done | bytes 360480 | tf_op jit(solution)/shard_map/ppermute | solution.py:383
  71.9 2.1 %collective-permute-start.14 = (bf16[4,2,96,128]{3,2,1,0:T(8,128)(2,1)S(1)}, bf16[4,2,96,128]{3,2,1,0:T(8,128)(2,1)S(1)}, u32[]{:S(2)}, u32[]{:S(2)}) collective-permute-start(bf16[4,2,96,128]{3,2,1,0:T(8,128)(2,1)S(1)} %slice.56), channel_id=1, source_target_pairs={{0,8},{8,16},{16,24},{24,32},{32,40},{40,48},{48,56},{56,0},{1,9},... | collective-permute-start | bytes 589832 | tf_op jit(solution)/shard_map/ppermute | solution.py:383
  74.0 3.2 %collective-permute-done.15.refs_13_ = bf16[4,2,80,128]{3,2,1,0:T(8,128)(2,1)S(1)} collective-permute-done((bf16[4,2,80,128]{3,2,1,0:T(8,128)(2,1)S(1)}, bf16[4,2,80,128]{3,2,1,0:T(8,128)(2,1)S(1)}, u32[]{:S(2)}, u32[]{:S(2)}) %collective-permute-start.15) | collective-permute-done | bytes 163872 | tf_op jit(solution)/shard_map/ppermute | solution.py:388
  77.2 1.7 collective-permute-done.14.refs_12_
  80.6 1.6 collective-permute-start.3
  84.5 7.3 %collective-permute-done.3.refs_3_ = bf16[8,2,96,128]{3,2,1,0:T(8,128)(2,1)} collective-permute-done((bf16[8,2,96,128]{3,2,1,0:T(8,128)(2,1)S(1)}, bf16[8,2,96,128]{3,2,1,0:T(8,128)(2,1)}, u32[]{:S(2)}, u32[]{:S(2)}) %collective-permute-start.3) | collective-permute-done | bytes 393248 | tf_op jit(solution)/shard_map/ppermute | solution.py:383
  91.8 2.3 %collective-permute-done.4.refs_4_ = bf16[8,2,80,128]{3,2,1,0:T(8,128)(2,1)} collective-permute-done((bf16[8,2,80,128]{3,2,1,0:T(8,128)(2,1)S(1)}, bf16[8,2,80,128]{3,2,1,0:T(8,128)(2,1)}, u32[]{:S(2)}, u32[]{:S(2)}) %collective-permute-start.4) | collective-permute-done | bytes 327712 | tf_op jit(solution)/shard_map/ppermute | solution.py:388
  94.3 1.9 %collective-permute-done.20.refs_18_ = bf16[8,2,80,128]{3,2,1,0:T(8,128)(2,1)} collective-permute-done((bf16[8,2,80,128]{3,2,1,0:T(8,128)(2,1)}, bf16[8,2,80,128]{3,2,1,0:T(8,128)(2,1)}, u32[]{:S(2)}, u32[]{:S(2)}) %collective-permute-start.20) | collective-permute-done | bytes 327712 | tf_op jit(solution)/shard_map/ppermute | solution.py:392
  96.3 36.3 %rows_work.1 = bf16[4,1312,128]{2,1,0:T(8,128)(2,1)} custom-call(s32[128]{0:T(128)} %order_ref.3, bf16[8,2,176,128]{3,2,1,0:T(8,128)(2,1)} %copy-done.1, bf16[8,2,176,128]{3,2,1,0:T(8,128)(2,1)} %collective-permute-done.1.refs_1_, bf16[8,2,176,128]{3,2,1,0:T(8,128)(2,1)} %collective-permute-done.2.refs_2_, ...), custom_call_target="tpu_custom_call" | custom-call | tf_op jit(solution)/shard_map/rows_work/pallas_call | solution.py:299
  132.6 23.2 %all_to_all.20.got_ref = bf16[4,1312,128]{2,1,0:T(8,128)(2,1)} all-to-all(bf16[4,1312,128]{2,1,0:T(8,128)(2,1)} %rows_work.1), channel_id=1, replica_groups=mesh['ctx_0'=4,'ctx_1'=8,'ctx_2'=2,'head'=4] {'head'}, dimensions={0} | all-to-all | bytes 2686976 | tf_op jit(solution)/shard_map/all_to_all | solution.py:370
  155.8 2.5 %spread_keys.1 = bf16[64,32,128]{2,1,0:T(8,128)(2,1)} custom-call(s32[128]{0:T(128)} %order_ref.3, bf16[4,1312,128]{2,1,0:T(8,128)(2,1)} %all_to_all.20.got_ref), custom_call_target="tpu_custom_call" | custom-call | tf_op jit(solution)/shard_map/spread_keys/pallas_call | solution.py:347
  158.3 9.9 %all-to-all-start.3 = ((bf16[64,32,128]{2,1,0:T(8,128)(2,1)}), bf16[64,32,128]{2,1,0:T(8,128)(2,1)S(1)}, u32[]{:S(2)}, u32[]{:S(2)}) async-start(bf16[64,32,128]{2,1,0:T(8,128)(2,1)} %spread_keys.1), calls=%async_computation.3 | async-start | bytes 1048576 | tf_op jit(solution)/shard_map/all_to_all | solution.py:371
  170.5 14.4 %all-to-all-done.3 = bf16[64,32,128]{2,1,0:T(8,128)(2,1)S(1)} async-done(((bf16[64,32,128]{2,1,0:T(8,128)(2,1)}), bf16[64,32,128]{2,1,0:T(8,128)(2,1)S(1)}, u32[]{:S(2)}, u32[]{:S(2)}) %all-to-all-start.3) | async-done | bytes 524320 | tf_op jit(solution)/shard_map/all_to_all | solution.py:371
  (92 shorter events, 13.3 us)
Async XLA Ops:
  3.2 6.9 %collective-permute-start.6 = (bf16[2,176,128]{2,1,0:T(8,128)(2,1)S(1)}, bf16[2,176,128]{2,1,0:T(8,128)(2,1)S(1)}, u32[]{:S(2)}, u32[]{:S(2)}) collective-permute-start(bf16[2,176,128]{2,1,0:T(8,128)(2,1)S(1)} %get-tuple-element.12), channel_id=1, source_target_pairs={{0,128},{64,192},{128,0},{192,64},{1,129},{65,193},{129,1},{193,65... | collective-permute-start | bytes 270344 | tf_op jit(solution)/shard_map/ppermute | solution.py:411
  5.5 5.8 %collective-permute-start.5 = (bf16[2,176,128]{2,1,0:T(8,128)(2,1)S(1)}, bf16[2,176,128]{2,1,0:T(8,128)(2,1)S(1)}, u32[]{:S(2)}, u32[]{:S(2)}) collective-permute-start(bf16[2,176,128]{2,1,0:T(8,128)(2,1)S(1)} %get-tuple-element.12), channel_id=1, source_target_pairs={{0,192},{64,0},{128,64},{192,128},{1,193},{65,1},{129,65},{193,129... | collective-permute-start | bytes 270344 | tf_op jit(solution)/shard_map/ppermute | solution.py:388
  6.9 4.6 %collective-permute-start.7 = (bf16[2,176,128]{2,1,0:T(8,128)(2,1)S(1)}, bf16[2,176,128]{2,1,0:T(8,128)(2,1)S(1)}, u32[]{:S(2)}, u32[]{:S(2)}) collective-permute-start(bf16[2,176,128]{2,1,0:T(8,128)(2,1)S(1)} %get-tuple-element.12), channel_id=1, source_target_pairs={{0,64},{64,128},{128,192},{192,0},{1,65},{65,129},{129,193},{193,1... | collective-permute-start | bytes 270344 | tf_op jit(solution)/shard_map/ppermute | solution.py:383
  12.2 15.5 %collective-permute-start.8 = (bf16[4,2,176,128]{3,2,1,0:T(8,128)(2,1)}, bf16[4,2,176,128]{3,2,1,0:T(8,128)(2,1)}, u32[]{:S(2)}, u32[]{:S(2)}) collective-permute-start(bf16[4,2,176,128]{3,2,1,0:T(8,128)(2,1)} %pad_maximum_fusion.1.refs_5_), channel_id=1, source_target_pairs={{0,56},{8,0},{16,8},{24,16},{32,24},{40,32},{48,40},{56,48},{1,57}... | collective-permute-start | bytes 1081352 | tf_op jit(solution)/shard_map/ppermute | solution.py:388
  21.0 25.1 %all-to-all-start = ((bf16[8,2,176,128]{3,2,1,0:T(8,128)(2,1)}), bf16[8,2,176,128]{3,2,1,0:T(8,128)(2,1)S(1)}, u32[]{:S(2)}, u32[]{:S(2)}) async-start(bf16[8,2,176,128]{3,2,1,0:T(8,128)(2,1)} %broadcast_in_dim.3), calls=%async_computation | async-start | bytes 1441792 | tf_op jit(solution)/shard_map/all_to_all | solution.py:397
  24.5 26.7 %collective-permute-start.11 = (bf16[4,2,176,128]{3,2,1,0:T(8,128)(2,1)}, bf16[4,2,176,128]{3,2,1,0:T(8,128)(2,1)}, u32[]{:S(2)}, u32[]{:S(2)}) collective-permute-start(bf16[4,2,176,128]{3,2,1,0:T(8,128)(2,1)} %pad_maximum_fusion.1.refs_5_), channel_id=1, source_target_pairs={{0,8},{8,16},{16,24},{24,32},{32,40},{40,48},{48,56},{56,0},{1,9},... | collective-permute-start | bytes 1081352 | tf_op jit(solution)/shard_map/ppermute | solution.py:383
  27.7 25.1 %collective-permute-start.9 = (bf16[4,2,176,128]{3,2,1,0:T(8,128)(2,1)}, bf16[4,2,176,128]{3,2,1,0:T(8,128)(2,1)}, u32[]{:S(2)}, u32[]{:S(2)}) collective-permute-start(bf16[4,2,176,128]{3,2,1,0:T(8,128)(2,1)} %collective-permute-done.8.refs_6_), channel_id=1, source_target_pairs={{0,56},{8,0},{16,8},{24,16},{32,24},{40,32},{48,40},{56,48},{1,57}... | collective-permute-start | bytes 1081352 | tf_op jit(solution)/shard_map/ppermute | solution.py:388
  46.0 48.2 %all-to-all-start.1 = ((bf16[4,2,16,10368]{3,2,1,0:T(8,128)(2,1)}), bf16[4,2,16,10368]{3,2,1,0:T(8,128)(2,1)S(1)}, u32[]{:S(2)}, u32[]{:S(2)}) async-start(bf16[4,2,16,10368]{3,2,1,0:T(8,128)(2,1)} %copy_bitcast_fusion), calls=%async_computation.1 | async-start | bytes 5308416 | tf_op jit(solution)/shard_map/all_to_all | solution.py:367
  51.2 10.9 %collective-permute-start.12 = (bf16[4,2,176,128]{3,2,1,0:T(8,128)(2,1)}, bf16[4,2,176,128]{3,2,1,0:T(8,128)(2,1)S(1)}, u32[]{:S(2)}, u32[]{:S(2)}) collective-permute-start(bf16[4,2,176,128]{3,2,1,0:T(8,128)(2,1)} %collective-permute-done.11.refs_11_), channel_id=1, source_target_pairs={{0,8},{8,16},{16,24},{24,32},{32,40},{40,48},{48,56},{56,0},{1,9},... | collective-permute-start | bytes 1081352 | tf_op jit(solution)/shard_map/ppermute | solution.py:383
  52.3 9.8 %collective-permute-start.21 = (bf16[4,2,176,128]{3,2,1,0:T(8,128)(2,1)}, bf16[4,2,176,128]{3,2,1,0:T(8,128)(2,1)S(1)}, u32[]{:S(2)}, u32[]{:S(2)}) collective-permute-start(bf16[4,2,176,128]{3,2,1,0:T(8,128)(2,1)} %pad_maximum_fusion.1.refs_5_), channel_id=1, source_target_pairs={{0,4},{4,0},{1,5},{5,1},{2,6},{6,2},{3,7},{7,3},{8,12},{12,8},{9,1... | collective-permute-start | bytes 1081352 | tf_op jit(solution)/shard_map/ppermute | solution.py:392
  52.3 11.4 %collective-permute-start.27 = (bf16[4,2,176,128]{3,2,1,0:T(8,128)(2,1)}, bf16[4,2,176,128]{3,2,1,0:T(8,128)(2,1)S(1)}, u32[]{:S(2)}, u32[]{:S(2)}) collective-permute-start(bf16[4,2,176,128]{3,2,1,0:T(8,128)(2,1)} %collective-permute-done.11.refs_11_), channel_id=1, source_target_pairs={{0,4},{4,0},{1,5},{5,1},{2,6},{6,2},{3,7},{7,3},{8,12},{12,8},{9,1... | collective-permute-start | bytes 1081352 | tf_op jit(solution)/shard_map/ppermute | solution.py:392
  52.8 10.9 %collective-permute-start.22 = (bf16[4,2,176,128]{3,2,1,0:T(8,128)(2,1)}, bf16[4,2,176,128]{3,2,1,0:T(8,128)(2,1)S(1)}, u32[]{:S(2)}, u32[]{:S(2)}) collective-permute-start(bf16[4,2,176,128]{3,2,1,0:T(8,128)(2,1)} %collective-permute-done.8.refs_6_), channel_id=1, source_target_pairs={{0,4},{4,0},{1,5},{5,1},{2,6},{6,2},{3,7},{7,3},{8,12},{12,8},{9,1... | collective-permute-start | bytes 1081352 | tf_op jit(solution)/shard_map/ppermute | solution.py:392
  52.8 11.4 %collective-permute-start.10 = (bf16[4,2,176,128]{3,2,1,0:T(8,128)(2,1)}, bf16[4,2,176,128]{3,2,1,0:T(8,128)(2,1)S(1)}, u32[]{:S(2)}, u32[]{:S(2)}) collective-permute-start(bf16[4,2,176,128]{3,2,1,0:T(8,128)(2,1)} %collective-permute-done.9.refs_7_), channel_id=1, source_target_pairs={{0,56},{8,0},{16,8},{24,16},{32,24},{40,32},{48,40},{56,48},{1,57}... | collective-permute-start | bytes 1081352 | tf_op jit(solution)/shard_map/ppermute | solution.py:388
  62.1 9.8 %collective-permute-start.13 = (bf16[4,2,176,128]{3,2,1,0:T(8,128)(2,1)S(1)}, bf16[4,2,176,128]{3,2,1,0:T(8,128)(2,1)S(1)}, u32[]{:S(2)}, u32[]{:S(2)}) collective-permute-start(bf16[4,2,176,128]{3,2,1,0:T(8,128)(2,1)S(1)} %collective-permute-done.12.refs_10_), channel_id=1, source_target_pairs={{0,8},{8,16},{16,24},{24,32},{32,40},{40,48},{48,56},{56,0},{1,9},... | collective-permute-start | bytes 1081352 | tf_op jit(solution)/shard_map/ppermute | solution.py:383
  62.1 16.8 %collective-permute-start.2 = (bf16[8,2,176,128]{3,2,1,0:T(8,128)(2,1)S(1)}, bf16[8,2,176,128]{3,2,1,0:T(8,128)(2,1)}, u32[]{:S(2)}, u32[]{:S(2)}) collective-permute-start(bf16[8,2,176,128]{3,2,1,0:T(8,128)(2,1)S(1)} %all-to-all-done.refs_0_), channel_id=1, source_target_pairs={{0,64},{64,128},{128,192},{192,0},{1,65},{65,129},{129,193},{193,1... | collective-permute-start | bytes 2162696 | tf_op jit(solution)/shard_map/ppermute | solution.py:383
  63.7 8.2 %collective-permute-start.26 = (bf16[4,2,176,128]{3,2,1,0:T(8,128)(2,1)S(1)}, bf16[4,2,176,128]{3,2,1,0:T(8,128)(2,1)S(1)}, u32[]{:S(2)}, u32[]{:S(2)}) collective-permute-start(bf16[4,2,176,128]{3,2,1,0:T(8,128)(2,1)S(1)} %collective-permute-done.12.refs_10_), channel_id=1, source_target_pairs={{0,4},{4,0},{1,5},{5,1},{2,6},{6,2},{3,7},{7,3},{8,12},{12,8},{9,1... | collective-permute-start | bytes 1081352 | tf_op jit(solution)/shard_map/ppermute | solution.py:392
  63.7 10.3 %collective-permute-start.23 = (bf16[4,2,176,128]{3,2,1,0:T(8,128)(2,1)}, bf16[4,2,176,128]{3,2,1,0:T(8,128)(2,1)S(1)}, u32[]{:S(2)}, u32[]{:S(2)}) collective-permute-start(bf16[4,2,176,128]{3,2,1,0:T(8,128)(2,1)} %collective-permute-done.9.refs_7_), channel_id=1, source_target_pairs={{0,4},{4,0},{1,5},{5,1},{2,6},{6,2},{3,7},{7,3},{8,12},{12,8},{9,1... | collective-permute-start | bytes 1081352 | tf_op jit(solution)/shard_map/ppermute | solution.py:392
  64.2 18.6 %collective-permute-start.1 = (bf16[8,2,176,128]{3,2,1,0:T(8,128)(2,1)S(1)}, bf16[8,2,176,128]{3,2,1,0:T(8,128)(2,1)}, u32[]{:S(2)}, u32[]{:S(2)}) collective-permute-start(bf16[8,2,176,128]{3,2,1,0:T(8,128)(2,1)S(1)} %all-to-all-done.refs_0_), channel_id=1, source_target_pairs={{0,192},{64,0},{128,64},{192,128},{1,193},{65,1},{129,65},{193,129... | collective-permute-start | bytes 2162696 | tf_op jit(solution)/shard_map/ppermute | solution.py:388
  71.9 5.3 %collective-permute-start.15 = (bf16[4,2,80,128]{3,2,1,0:T(8,128)(2,1)S(1)}, bf16[4,2,80,128]{3,2,1,0:T(8,128)(2,1)S(1)}, u32[]{:S(2)}, u32[]{:S(2)}) collective-permute-start(bf16[4,2,80,128]{3,2,1,0:T(8,128)(2,1)S(1)} %slice.57), channel_id=1, source_target_pairs={{0,56},{8,0},{16,8},{24,16},{32,24},{40,32},{48,40},{56,48},{1,57}... | collective-permute-start | bytes 491528 | tf_op jit(solution)/shard_map/ppermute | solution.py:388
  71.9 7.0 %collective-permute-start.14 = (bf16[4,2,96,128]{3,2,1,0:T(8,128)(2,1)S(1)}, bf16[4,2,96,128]{3,2,1,0:T(8,128)(2,1)S(1)}, u32[]{:S(2)}, u32[]{:S(2)}) collective-permute-start(bf16[4,2,96,128]{3,2,1,0:T(8,128)(2,1)S(1)} %slice.56), channel_id=1, source_target_pairs={{0,8},{8,16},{16,24},{24,32},{32,40},{40,48},{48,56},{56,0},{1,9},... | collective-permute-start | bytes 589832 | tf_op jit(solution)/shard_map/ppermute | solution.py:383
  74.0 8.2 %collective-permute-start.25 = (bf16[4,2,176,128]{3,2,1,0:T(8,128)(2,1)S(1)}, bf16[4,2,176,128]{3,2,1,0:T(8,128)(2,1)S(1)}, u32[]{:S(2)}, u32[]{:S(2)}) collective-permute-start(bf16[4,2,176,128]{3,2,1,0:T(8,128)(2,1)S(1)} %collective-permute-done.13.refs_9_), channel_id=1, source_target_pairs={{0,4},{4,0},{1,5},{5,1},{2,6},{6,2},{3,7},{7,3},{8,12},{12,8},{9,1... | collective-permute-start | bytes 1081352 | tf_op jit(solution)/shard_map/ppermute | solution.py:392
  77.2 5.1 %collective-permute-start.24 = (bf16[4,2,176,128]{3,2,1,0:T(8,128)(2,1)S(1)}, bf16[4,2,176,128]{3,2,1,0:T(8,128)(2,1)S(1)}, u32[]{:S(2)}, u32[]{:S(2)}) collective-permute-start(bf16[4,2,176,128]{3,2,1,0:T(8,128)(2,1)S(1)} %collective-permute-done.10.refs_8_), channel_id=1, source_target_pairs={{0,4},{4,0},{1,5},{5,1},{2,6},{6,2},{3,7},{7,3},{8,12},{12,8},{9,1... | collective-permute-start | bytes 1081352 | tf_op jit(solution)/shard_map/ppermute | solution.py:392
  78.9 1.7 collective-permute-start.29
  78.9 5.0 %collective-permute-start.28 = (bf16[4,2,96,128]{3,2,1,0:T(8,128)(2,1)S(1)}, bf16[4,2,96,128]{3,2,1,0:T(8,128)(2,1)S(1)}, u32[]{:S(2)}, u32[]{:S(2)}) collective-permute-start(bf16[4,2,96,128]{3,2,1,0:T(8,128)(2,1)S(1)} %collective-permute-done.14.refs_12_), channel_id=1, source_target_pairs={{0,4},{4,0},{1,5},{5,1},{2,6},{6,2},{3,7},{7,3},{8,12},{12,8},{9,1... | collective-permute-start | bytes 589832 | tf_op jit(solution)/shard_map/ppermute | solution.py:392
  80.6 11.2 %collective-permute-start.3 = (bf16[8,2,96,128]{3,2,1,0:T(8,128)(2,1)S(1)}, bf16[8,2,96,128]{3,2,1,0:T(8,128)(2,1)}, u32[]{:S(2)}, u32[]{:S(2)}) collective-permute-start(bf16[8,2,96,128]{3,2,1,0:T(8,128)(2,1)S(1)} %slice.54), channel_id=1, source_target_pairs={{0,64},{64,128},{128,192},{192,0},{1,65},{65,129},{129,193},{193,1... | collective-permute-start | bytes 1179656 | tf_op jit(solution)/shard_map/ppermute | solution.py:383
  82.2 12.1 %collective-permute-start.16 = (bf16[8,2,176,128]{3,2,1,0:T(8,128)(2,1)S(1)}, bf16[8,2,176,128]{3,2,1,0:T(8,128)(2,1)}, u32[]{:S(2)}, u32[]{:S(2)}) collective-permute-start(bf16[8,2,176,128]{3,2,1,0:T(8,128)(2,1)S(1)} %all-to-all-done.refs_0_), channel_id=1, source_target_pairs={{0,4},{4,0},{1,5},{5,1},{2,6},{6,2},{3,7},{7,3},{8,12},{12,8},{9,1... | collective-permute-start | bytes 2162696 | tf_op jit(solution)/shard_map/ppermute | solution.py:392
  82.3 13.9 %collective-permute-start.18 = (bf16[8,2,176,128]{3,2,1,0:T(8,128)(2,1)}, bf16[8,2,176,128]{3,2,1,0:T(8,128)(2,1)}, u32[]{:S(2)}, u32[]{:S(2)}) collective-permute-start(bf16[8,2,176,128]{3,2,1,0:T(8,128)(2,1)} %collective-permute-done.2.refs_2_), channel_id=1, source_target_pairs={{0,4},{4,0},{1,5},{5,1},{2,6},{6,2},{3,7},{7,3},{8,12},{12,8},{9,1... | collective-permute-start | bytes 2162696 | tf_op jit(solution)/shard_map/ppermute | solution.py:392
  82.8 13.4 %collective-permute-start.17 = (bf16[8,2,176,128]{3,2,1,0:T(8,128)(2,1)}, bf16[8,2,176,128]{3,2,1,0:T(8,128)(2,1)}, u32[]{:S(2)}, u32[]{:S(2)}) collective-permute-start(bf16[8,2,176,128]{3,2,1,0:T(8,128)(2,1)} %collective-permute-done.1.refs_1_), channel_id=1, source_target_pairs={{0,4},{4,0},{1,5},{5,1},{2,6},{6,2},{3,7},{7,3},{8,12},{12,8},{9,1... | collective-permute-start | bytes 2162696 | tf_op jit(solution)/shard_map/ppermute | solution.py:392
  83.9 10.2 %collective-permute-start.4 = (bf16[8,2,80,128]{3,2,1,0:T(8,128)(2,1)S(1)}, bf16[8,2,80,128]{3,2,1,0:T(8,128)(2,1)}, u32[]{:S(2)}, u32[]{:S(2)}) collective-permute-start(bf16[8,2,80,128]{3,2,1,0:T(8,128)(2,1)S(1)} %slice.55), channel_id=1, source_target_pairs={{0,192},{64,0},{128,64},{192,128},{1,193},{65,1},{129,65},{193,129... | collective-permute-start | bytes 983048 | tf_op jit(solution)/shard_map/ppermute | solution.py:388
  91.8 4.4 %collective-permute-start.19 = (bf16[8,2,96,128]{3,2,1,0:T(8,128)(2,1)}, bf16[8,2,96,128]{3,2,1,0:T(8,128)(2,1)}, u32[]{:S(2)}, u32[]{:S(2)}) collective-permute-start(bf16[8,2,96,128]{3,2,1,0:T(8,128)(2,1)} %collective-permute-done.3.refs_3_), channel_id=1, source_target_pairs={{0,4},{4,0},{1,5},{5,1},{2,6},{6,2},{3,7},{7,3},{8,12},{12,8},{9,1... | collective-permute-start | bytes 1179656 | tf_op jit(solution)/shard_map/ppermute | solution.py:392
  94.2 2.1 %collective-permute-start.20 = (bf16[8,2,80,128]{3,2,1,0:T(8,128)(2,1)}, bf16[8,2,80,128]{3,2,1,0:T(8,128)(2,1)}, u32[]{:S(2)}, u32[]{:S(2)}) collective-permute-start(bf16[8,2,80,128]{3,2,1,0:T(8,128)(2,1)} %collective-permute-done.4.refs_4_), channel_id=1, source_target_pairs={{0,4},{4,0},{1,5},{5,1},{2,6},{6,2},{3,7},{7,3},{8,12},{12,8},{9,1... | collective-permute-start | bytes 983048 | tf_op jit(solution)/shard_map/ppermute | solution.py:392
  158.3 26.5 %all-to-all-start.3 = ((bf16[64,32,128]{2,1,0:T(8,128)(2,1)}), bf16[64,32,128]{2,1,0:T(8,128)(2,1)S(1)}, u32[]{:S(2)}, u32[]{:S(2)}) async-start(bf16[64,32,128]{2,1,0:T(8,128)(2,1)} %spread_keys.1), calls=%async_computation.3 | async-start | bytes 1048576 | tf_op jit(solution)/shard_map/all_to_all | solution.py:371
  (19 other events, 293.0 us)
